TPU v7x, 8 devices: a whole 2x2x1 slice. The times are simulated.
8 devices in a mesh: rep: 1 (over z), r: 2 (over y), s: 4 (over x, core).
Axes of the slice: x: 2, y: 2, z: 1, core: 2. Of those that a mesh axis runs over, the one named last changes fastest.
Arguments:
- x: bfloat16 [8, 4096, 896], P(('rep', 'r', 's'))
- dy: bfloat16 [8, 4096, 896], P(('rep', 'r', 's'))
- w_gate: bfloat16 [2, 896, 2304], P(None, 's')
- w_up: bfloat16 [2, 896, 2304], P(None, 's')
- w_down: bfloat16 [2, 2304, 896], P(None, 's')
- m_w_gate: float32 [2, 896, 2304], P(None, 's')
- m_w_up: float32 [2, 896, 2304], P(None, 's')
- m_w_down: float32 [2, 2304, 896], P(None, 's')
- v_w_gate: float32 [2, 896, 2304], P(None, 's')
- v_w_up: float32 [2, 896, 2304], P(None, 's')
- v_w_down: float32 [2, 2304, 896], P(None, 's')
Outputs:
- output 1: bfloat16 [2, 896, 2304], P('rep', 's')
- output 2: bfloat16 [2, 896, 2304], P('rep', 's')
- output 3: bfloat16 [2, 2304, 896], P('rep', 's')
- output 4: float32 [2, 896, 2304], P('rep', 's')
- output 5: float32 [2, 896, 2304], P('rep', 's')
- output 6: float32 [2, 2304, 896], P('rep', 's')
- output 7: float32 [2, 896, 2304], P('rep', 's')
- output 8: float32 [2, 896, 2304], P('rep', 's')
- output 9: float32 [2, 2304, 896], P('rep', 's')
All inputs are finite; a program needn't handle non-finite values.
Results may differ from a plain program's by a relative error of at most 0.022.
Values are sent between devices in bfloat16 or wider.
A program may use at most 2 GiB of HBM per device.

v0:
```python
import jax
import jax.numpy as jnp
from jax import lax
from jax.sharding import PartitionSpec as P

NAMES = ("w_gate", "w_up", "w_down")


def matmul(a, w):
    return jnp.dot(a, w, preferred_element_type=jnp.float32).astype(jnp.bfloat16)


def normed(h):
    wide = h.astype(jnp.float32)
    scale = lax.rsqrt(jnp.mean(wide**2, -1, keepdims=True) + 1e-6)
    return (wide * scale).astype(jnp.bfloat16)


def layer(h, w):
    a = normed(h)
    gate = jnp.dot(a, w["w_gate"], preferred_element_type=jnp.float32)
    up = jnp.dot(a, w["w_up"], preferred_element_type=jnp.float32)
    return h + matmul((jax.nn.silu(gate) * up).astype(jnp.bfloat16), w["w_down"])


def adamw(w, m, v, g):
    m = 0.9 * m + 0.1 * g
    v = 0.95 * v + 0.05 * g * g
    step = m * lax.rsqrt(v + 1e-8) + 0.1 * w
    return (w - 0.02 * step).astype(jnp.bfloat16), m, v


def clipped(gradients, sum_of_squares, count):
    factor = jnp.minimum(1.0, 0.5 * lax.rsqrt(sum_of_squares / count + 1e-30))
    return [g * factor for g in gradients]


def solution(mesh):
    def fetched(weights, number):
        return {name: lax.all_gather(w[number], "s", axis=0, tiled=True) for name, w in zip(NAMES, weights, strict=True)}

    def summed(term):
        return lax.psum(lax.psum_scatter(term, "s", scatter_dimension=0, tiled=True), "r")

    def step(x, dy, *arrays):
        weights, m, v = (arrays[i : i + 3] for i in (0, 3, 6))
        layers = weights[0].shape[0]
        h, kept = x[0], []
        for number in range(layers):
            kept.append(h)
            h = layer(h, fetched(weights, number))
        by_h, mine = dy[0], [None] * layers
        for number in reversed(range(layers)):
            _, back = jax.vjp(lambda w, h: layer(h, w), fetched(weights, number), kept[number])
            by_w, by_h = back(by_h)
            mine[number] = [summed(by_w[name]) for name in NAMES]
        gradients = [jnp.stack([mine[number][i] for number in range(layers)]).astype(jnp.float32) for i in range(3)]
        squares = lax.psum(sum(jnp.sum(g * g) for g in gradients), "s")
        gradients = clipped(gradients, squares, lax.psum(1, "s") * sum(g.size for g in gradients))
        new = [adamw(w.astype(jnp.float32), m, v, g) for w, m, v, g in zip(weights, m, v, gradients, strict=True)]
        return tuple(one[which] for which in range(3) for one in new)

    states, cut = P(("rep", "r", "s"), None, None), P(None, "s", None)
    return jax.shard_map(
        step,
        mesh=mesh,
        in_specs=(states, states) + (cut,) * 9,
        out_specs=(P("rep", "s", None),) * 9,
        check_vma=False,
    )
```

profile of v0, /device:TPU:0, one launch (start us, length us, event | category | flops | bytes accessed | tf_op | source)
XLA Modules:
  0.0 811.6 jit_solution(18115973855635915284)
XLA Ops:
  16.7 10.8 %copy.20 = bf16[1,4096,896]{1,2,0:T(8,128)(2,1)} copy(bf16[1,4096,896]{2,1,0:T(8,128)(2,1)} %param.11) | data formatting | bytes 14680064 | tf_op args[0]
  32.1 10.7 %copy.21 = bf16[1,4096,896]{1,2,0:T(8,128)(2,1)} copy(bf16[1,4096,896]{2,1,0:T(8,128)(2,1)} %param.12) | data formatting | bytes 14680064 | tf_op args[1]
  44.5 27.0 %fusion.47 = f32[4096,2304]{1,0:T(8,128)} fusion(bf16[1,4096,896]{1,2,0:T(8,128)(2,1)} %copy.20, f32[4096]{0:T(1024)S(1)} %add_rsqrt_fusion, bf16[1,896,2304]{2,1,0:T(8,128)(2,1)} %all-gather.13.cloned.1.call-done), kind=kOutput, calls=%fused_computation.72 | convolution fusion | flops 16922443776 | bytes 49233920 | tf_op jit(solution)/shard_map/dot_general | solution.py:21
  77.7 41.9 %multiply_convert_fusion.1 = (bf16[4096,2304]{1,0:T(8,128)(2,1)}, f32[4096,2304]{1,0:T(8,128)}) fusion(f32[4096,2304]{1,0:T(8,128)} %fusion.47, bf16[1,896,2304]{2,1,0:T(8,128)(2,1)} %all-gather.15.cloned.1.call-done, bf16[1,4096,896]{1,2,0:T(8,128)(2,1)} %copy.20, f32[4096]{0:T(1024)S(1)} %add_rsqrt_fusion), kind=kOutput, calls=%fused_computation.17 | convolution fusion | flops 16979066880 | bytes 105857024 | tf_op jit(solution)/shard_map/dot_general | solution.py:22
  119.7 24.4 %fusion.19 = (f32[4096]{0:T(1024)S(1)}, bf16[4096,896]{0,1:T(8,128)(2,1)}) fusion(bf16[4096,2304]{1,0:T(8,128)(2,1)} %get-tuple-element.30, bf16[1,2304,896]{2,1,0:T(8,128)(2,1)} %all-gather.17.cloned.1.call-done, bf16[1,4096,896]{1,2,0:T(8,128)(2,1)} %copy.20), kind=kOutput, calls=%fused_computation.37 | convolution fusion | flops 16929779712 | bytes 37699584 | tf_op jit(solution)/shard_map/dot_general | solution.py:10
  144.8 27.1 %fusion.39 = f32[4096,2304]{1,0:T(8,128)} fusion(bf16[4096,896]{0,1:T(8,128)(2,1)} %get-tuple-element.33, f32[4096]{0:T(1024)S(1)} %fusion.77, bf16[1,896,2304]{2,1,0:T(8,128)(2,1)} %all-gather.23.cloned.1.call-done), kind=kOutput, calls=%fused_computation.69 | convolution fusion | flops 16922443776 | bytes 49233920 | tf_op jit(solution)/shard_map/jvp()/dot_general | solution.py:22
  177.2 26.5 %convolution_convert_fusion.1 = bf16[4096,2304]{1,0:T(8,128)(2,1)} fusion(bf16[1,4096,896]{2,1,0:T(8,128)(2,1)} %param.12, bf16[1,2304,896]{2,1,0:T(8,128)(2,1)} %all-gather.21.cloned.1.call-done), kind=kOutput, calls=%fused_computation.27 | convolution fusion | flops 16920870912 | bytes 30343168 | tf_op jit(solution)/shard_map/transpose(jvp())/dot_general | solution.py:10
  210.3 52.3 %fusion.2 = (bf16[4096,2304]{1,0:T(8,128)(2,1)}, f32[4096,2304]{1,0:T(8,128)}) fusion(f32[4096,2304]{1,0:T(8,128)} %fusion.39, bf16[4096,2304]{1,0:T(8,128)(2,1)} %convolution_convert_fusion.1, bf16[1,896,2304]{2,1,0:T(8,128)(2,1)} %all-gather.19.cloned.1.call-done, bf16[4096,896]{0,1:T(8,128)(2,1)} %get-tuple-element.33, f32[4096]{0:T(1024)S(1)} %fusion.77), kind=kOutput, calls=%fused_computation.8 | convolution fusion | flops 17035689984 | bytes 124731392 | tf_op jit(solution)/shard_map/jvp()/dot_general | solution.py:21
  262.6 22.8 %fusion.70 = bf16[4096,896]{0,1:T(8,128)(2,1)} fusion(bf16[4096,2304]{1,0:T(8,128)(2,1)} %get-tuple-element.34, bf16[1,896,2304]{2,1,0:T(8,128)(2,1)} %all-gather.19.cloned.1.call-done), kind=kOutput, calls=%fused_computation.94 | convolution fusion | flops 16911433728 | bytes 30343168 | tf_op jit(solution)/shard_map/transpose(jvp())/dot_general | solution.py:21
  285.4 35.3 %fusion.21 = (f32[4096]{0:T(1024)S(1)}, bf16[4096,896]{0,1:T(8,128)(2,1)}) fusion(bf16[4096,896]{0,1:T(8,128)(2,1)} %get-tuple-element.33, bf16[4096,896]{0,1:T(8,128)(2,1)} %fusion.70, bf16[1,896,2304]{2,1,0:T(8,128)(2,1)} %all-gather.23.cloned.1.call-done, bf16[4096,2304]{1,0:T(8,128)(2,1)} %convolution_convert_fusion.1, f32[4096,2304]{1,0:T(8,128)} %get-tuple-element.35), kind=kOutput, calls=%fused_computation.39 | convolution fusion | flops 16990072832 | bytes 82788352 | tf_op jit(solution)/shard_map/transpose(jvp())/dot_general | solution.py:22
  320.7 9.8 %fusion.22 = bf16[4096,896]{0,1:T(8,128)(2,1)S(1)} fusion(bf16[4096,896]{0,1:T(8,128)(2,1)} %get-tuple-element.33, bf16[4096,896]{0,1:T(8,128)(2,1)} %get-tuple-element.37, bf16[1,4096,896]{1,2,0:T(8,128)(2,1)} %copy.21, f32[4096]{0:T(1024)S(1)} %multiply_multiply_fusion.3, f32[4096]{0:T(1024)S(1)} %fusion.77), kind=kLoop, calls=%fused_computation.40 | loop fusion | flops 25690112 | bytes 29392896 | tf_op jit(solution)/shard_map/transpose(jvp())/add_any | solution.py:14
  333.5 24.2 %convolution_convert_fusion.2 = bf16[2304,896]{1,0:T(8,128)(2,1)} fusion(bf16[4096,2304]{1,0:T(8,128)(2,1)} %get-tuple-element.30, bf16[4096,896]{0,1:T(8,128)(2,1)S(1)} %fusion.22), kind=kOutput, calls=%fused_computation.52 | convolution fusion | flops 16913498112 | bytes 30343168 | tf_op jit(solution)/shard_map/transpose(jvp())/dot_general | solution.py:10
  357.7 34.1 %fusion.26 = bf16[2304,896]{1,0:T(8,128)(2,1)} fusion(bf16[1,4096,896]{2,1,0:T(8,128)(2,1)} %param.12, f32[4096,2304]{1,0:T(8,128)} %fusion.39, f32[4096,2304]{1,0:T(8,128)} %get-tuple-element.35), kind=kOutput, calls=%fused_computation.48 | convolution fusion | flops 16970121216 | bytes 86966272 | tf_op jit(solution)/shard_map/transpose(jvp())/dot_general | solution.py:10
  391.9 27.4 %convolution_convert_fusion = bf16[4096,2304]{1,0:T(8,128)(2,1)} fusion(bf16[4096,896]{0,1:T(8,128)(2,1)} %copy-done.4, bf16[1,2304,896]{2,1,0:T(8,128)(2,1)} %all-gather.17.cloned.1.call-done), kind=kOutput, calls=%fused_computation.26 | convolution fusion | flops 16920870912 | bytes 30343168 | tf_op jit(solution)/shard_map/transpose(jvp())/dot_general | solution.py:10
  419.3 34.5 %fusion.33 = bf16[896,2304]{1,0:T(8,128)(2,1)} fusion(bf16[4096,2304]{1,0:T(8,128)(2,1)} %convolution_convert_fusion, f32[4096,2304]{1,0:T(8,128)} %fusion.47, bf16[1,4096,896]{1,2,0:T(8,128)(2,1)} %copy.20, f32[4096]{0:T(1024)S(1)} %copy-done.16), kind=kOutput, calls=%fused_computation.51 | convolution fusion | flops 16981131264 | bytes 68108288 | tf_op jit(solution)/shard_map/transpose(jvp())/dot_general | solution.py:22
  453.9 34.1 %fusion.29 = bf16[896,2304]{1,0:T(8,128)(2,1)} fusion(bf16[4096,2304]{1,0:T(8,128)(2,1)} %convolution_convert_fusion.1, bf16[4096,896]{0,1:T(8,128)(2,1)} %get-tuple-element.33, f32[4096]{0:T(1024)S(1)} %copy-done.12, f32[4096,2304]{1,0:T(8,128)} %get-tuple-element.35), kind=kOutput, calls=%fused_computation.49 | convolution fusion | flops 16981131264 | bytes 68108288 | tf_op jit(solution)/shard_map/transpose(jvp())/dot_general | solution.py:22
  488.0 39.4 %fusion.30 = bf16[896,2304]{1,0:T(8,128)(2,1)} fusion(f32[4096,2304]{1,0:T(8,128)} %fusion.47, f32[4096,2304]{1,0:T(8,128)} %get-tuple-element.31, bf16[4096,2304]{1,0:T(8,128)(2,1)} %convolution_convert_fusion, bf16[1,4096,896]{1,2,0:T(8,128)(2,1)} %copy.20, f32[4096]{0:T(1024)S(1)} %copy-done.16), kind=kOutput, calls=%fused_computation.50 | convolution fusion | flops 17028317184 | bytes 105857024 | tf_op jit(solution)/shard_map/transpose(jvp())/dot_general | solution.py:21
  527.4 23.8 %convolution_convert_fusion.3 = bf16[896,2304]{1,0:T(8,128)(2,1)} fusion(bf16[4096,2304]{1,0:T(8,128)(2,1)} %get-tuple-element.34, bf16[4096,896]{0,1:T(8,128)(2,1)} %get-tuple-element.33, f32[4096]{0:T(1024)S(1)} %copy-done.12), kind=kOutput, calls=%fused_computation.53 | convolution fusion | flops 16922443776 | bytes 30359552 | tf_op jit(solution)/shard_map/transpose(jvp())/dot_general | solution.py:21
  551.4 22.3 %reduce-scatter.7.cloned.1.call-done = bf16[224,2304]{1,0:T(8,128)(2,1)} async-done(((bf16[896,2304]{1,0:T(8,128)(2,1)}), bf16[224,2304]{1,0:T(8,128)(2,1)}) %reduce-scatter.7.cloned.1.call-update) | async-done | bytes 1032208 | tf_op jit(solution)/shard_map/reduce_scatter | solution.py:43
  573.7 40.9 %reduce-scatter.9.cloned.1.call-done = bf16[224,2304]{1,0:T(8,128)(2,1)} async-done(((bf16[896,2304]{1,0:T(8,128)(2,1)}), bf16[224,2304]{1,0:T(8,128)(2,1)}) %reduce-scatter.9.cloned.1.call-update) | async-done | bytes 1032208 | tf_op jit(solution)/shard_map/reduce_scatter | solution.py:43
  614.6 148.3 %all-reduce.3.cloned.1.call-done = (bf16[1,224,2304]{2,1,0:T(8,128)(2,1)}, bf16[1,224,2304]{2,1,0:T(8,128)(2,1)}, bf16[1,224,2304]{2,1,0:T(8,128)(2,1)}, bf16[1,...) async-done(((bf16[1,224,2304]{2,1,0:T(8,128)(2,1)}, bf16[1,224,2304]{2,1,0:T(8,128)(2,1)}, bf16[1,224,2304]{2,1,0:T(8,128)(2,1)}, ...) | async-done | bytes 6193168 | tf_op jit(solution)/shard_map/psum | solution.py:43
  774.4 6.8 psum.55
  782.0 9.0 %fusion.63 = (bf16[2,576,896]{2,1,0:T(8,128)(2,1)}, f32[2,576,896]{2,1,0:T(8,128)}, f32[2,576,896]{2,1,0:T(8,128)}) fusion(bf16[2,576,896]{2,1,0:T(8,128)(2,1)S(1)} %copy-done.1, f32[]{:T(128)S(6)} %min_shard_map.3, bf16[1,576,896]{2,1,0:T(8,128)(2,1)} %get-tuple-element.13, bf16[1,576,896]{2,1,0:T(8,128)(2,1)} %get-tuple-element.14, ...), kind=kLoop, calls=%fused_computation.87 | loop fusion | flops 20643840 | bytes 22708228 | tf_op jit(solution)/shard_map/convert_element_type | solution.py:30
  796.0 8.9 %fusion.54 = (bf16[2,224,2304]{2,1,0:T(8,128)(2,1)}, f32[2,224,2304]{2,1,0:T(8,128)}, f32[2,224,2304]{2,1,0:T(8,128)}, bf16[2,224,2304]{2,1,0:T(8,128)(2,1)}, f3...) fusion(bf16[2,224,2304]{2,1,0:T(8,128)(2,1)S(1)} %copy-done.2, f32[]{:T(128)S(6)} %min_shard_map.3, ...), kind=kLoop, calls=%fused_computation.78 | loop fusion | flops 41287680 | bytes 45416452 | tf_op jit(solution)/shard_map/convert_element_type | solution.py:30
  (80 shorter events, 52.6 us)
Async XLA Ops:
  7.2 37.3 %all-gather.13.cloned.1.call-start = ((), (), s32[]{:S(2)}) async-start(), calls=%async_computation.12 | async-start | bytes 5160960 | tf_op jit(solution)/shard_map/all_gather | solution.py:40
  10.4 67.4 %all-gather.15.cloned.1.call-start = ((), (), s32[]{:S(2)}) async-start(), calls=%async_computation.13 | async-start | bytes 5160960 | tf_op jit(solution)/shard_map/all_gather | solution.py:40
  13.4 106.3 %all-gather.17.cloned.1.call-start = ((), (), s32[]{:S(2)}) async-start(), calls=%async_computation.14 | async-start | bytes 5160960 | tf_op jit(solution)/shard_map/all_gather | solution.py:40
  15.0 129.8 %all-gather.23.cloned.1.call-start = ((), (), s32[]{:S(2)}) async-start(), calls=%async_computation.17 | async-start | bytes 5160960 | tf_op jit(solution)/shard_map/all_gather | solution.py:40
  15.5 161.7 %all-gather.21.cloned.1.call-start = ((), (), s32[]{:S(2)}) async-start(), calls=%async_computation.16 | async-start | bytes 5160960 | tf_op jit(solution)/shard_map/all_gather | solution.py:40
  16.1 194.2 %all-gather.19.cloned.1.call-start = ((), (), s32[]{:S(2)}) async-start(), calls=%async_computation.15 | async-start | bytes 5160960 | tf_op jit(solution)/shard_map/all_gather | solution.py:40
  16.7 534.6 %reduce-scatter.15.cloned.1.call-start = ((), (), s32[]{:S(2)}) async-start(), calls=%async_computation.10 | async-start | bytes 5160960 | tf_op jit(solution)/shard_map/reduce_scatter | solution.py:43
  32.1 45.6 %copy-start.15 = (f32[4096]{0:T(1024)}, f32[4096]{0:T(1024)S(1)}, u32[]{:S(2)}) copy-start(f32[4096]{0:T(1024)S(1)} %add_rsqrt_fusion) | copy-start | bytes 49156
  144.7 176.0 %copy-start.11 = (f32[4096]{0:T(1024)}, f32[4096]{0:T(1024)S(1)}, u32[]{:S(2)}) copy-start(f32[4096]{0:T(1024)S(1)} %fusion.77) | copy-start | bytes 49156
  285.4 35.3 %copy-start.14 = (f32[4096]{0:T(1024)S(1)}, f32[4096]{0:T(1024)}, u32[]{:S(2)}) copy-start(f32[4096]{0:T(1024)} %copy-done.13) | copy-start | bytes 49156
  357.7 193.6 %reduce-scatter.17.cloned.1.call-start = ((), (), s32[]{:S(2)}) async-start(), calls=%async_computation.11 | async-start | bytes 5160960 | tf_op jit(solution)/shard_map/reduce_scatter | solution.py:43
  391.8 27.5 %copy-start.16 = (f32[4096]{0:T(1024)S(1)}, f32[4096]{0:T(1024)}, u32[]{:S(2)}) copy-start(f32[4096]{0:T(1024)} %copy-done.15) | copy-start | bytes 49156
  391.8 159.5 %reduce-scatter.11.cloned.1.call-start = ((), (), s32[]{:S(2)}) async-start(), calls=%async_computation.8 | async-start | bytes 5160960 | tf_op jit(solution)/shard_map/reduce_scatter | solution.py:43
  419.3 34.5 %copy-start.12 = (f32[4096]{0:T(1024)S(1)}, f32[4096]{0:T(1024)}, u32[]{:S(2)}) copy-start(f32[4096]{0:T(1024)} %copy-done.11) | copy-start | bytes 49156
  453.8 97.6 %reduce-scatter.13.cloned.1.call-start = ((), (), s32[]{:S(2)}) async-start(), calls=%async_computation.9 | async-start | bytes 5160960 | tf_op jit(solution)/shard_map/reduce_scatter | solution.py:43
  487.9 85.8 %reduce-scatter.7.cloned.1.call-start = ((), (), s32[]{:S(2)}) async-start(), calls=%async_computation.6 | async-start | bytes 5160960 | tf_op jit(solution)/shard_map/reduce_scatter | solution.py:43
  527.4 87.2 %reduce-scatter.9.cloned.1.call-start = ((), (), s32[]{:S(2)}) async-start(), calls=%async_computation.7 | async-start | bytes 5160960 | tf_op jit(solution)/shard_map/reduce_scatter | solution.py:43
  551.2 230.7 %copy-start.1 = (bf16[2,576,896]{2,1,0:T(8,128)(2,1)S(1)}, bf16[2,576,896]{2,1,0:T(8,128)(2,1)}, u32[]{:S(2)}) copy-start(bf16[2,576,896]{2,1,0:T(8,128)(2,1)} %param.15) | copy-start | bytes 6193156
  551.2 211.7 %all-reduce.3.cloned.1.call-start = ((), (), s32[]{:S(2)}) async-start(), calls=%async_computation.18 | async-start | bytes 12386304 | tf_op jit(solution)/shard_map/psum | solution.py:43
  782.0 11.2 %copy-start.6 = (f32[2,224,2304]{2,1,0:T(8,128)S(1)}, f32[2,224,2304]{2,1,0:T(8,128)}, u32[]{:S(2)}) copy-start(f32[2,224,2304]{2,1,0:T(8,128)} %param.16) | copy-start | bytes 12386308
  782.0 12.3 %copy-start.7 = (f32[2,224,2304]{2,1,0:T(8,128)S(1)}, f32[2,224,2304]{2,1,0:T(8,128)}, u32[]{:S(2)}) copy-start(f32[2,224,2304]{2,1,0:T(8,128)} %param.20) | copy-start | bytes 12386308
  782.0 13.5 %copy-start.8 = (f32[2,224,2304]{2,1,0:T(8,128)S(1)}, f32[2,224,2304]{2,1,0:T(8,128)}, u32[]{:S(2)}) copy-start(f32[2,224,2304]{2,1,0:T(8,128)} %param.17) | copy-start | bytes 12386308
  782.0 13.7 %copy-start.9 = (bf16[1,224,2304]{2,1,0:T(8,128)(2,1)S(1)}, bf16[1,224,2304]{2,1,0:T(8,128)(2,1)}, u32[]{:S(2)}) copy-start(bf16[1,224,2304]{2,1,0:T(8,128)(2,1)} %get-tuple-element.9) | copy-start | bytes 3096580
  782.0 14.0 %copy-start.10 = (bf16[1,224,2304]{2,1,0:T(8,128)(2,1)S(1)}, bf16[1,224,2304]{2,1,0:T(8,128)(2,1)}, u32[]{:S(2)}) copy-start(bf16[1,224,2304]{2,1,0:T(8,128)(2,1)} %get-tuple-element.10) | copy-start | bytes 3096580
  (6 other events, 37.8 us)
Sparse Core Ops, SparseCore 0:
  10.5 33.9 all-gather.12
  46.6 31.1 all-gather.14
  79.8 31.1 all-gather.16
  113.0 31.1 all-gather.22
  146.1 31.1 all-gather.20
  179.2 31.1 all-gather.18
  357.8 37.8 reduce-scatter.14
  398.8 37.8 reduce-scatter.16
  453.9 37.8 reduce-scatter.10
  494.8 37.8 reduce-scatter.12
  535.8 37.8 reduce-scatter.6
  576.7 37.8 reduce-scatter.8
  617.6 145.2 all-reduce.2
where the time goes:
time: 818 us; the launch traced here: 812 us
  matrix products  475 us (58%)
  waiting for transfers between devices  233 us (28%)
  other arithmetic  41.8 us (5%)
  local copies, waits for them, and re-layouts  37.7 us (5%)
  between operations  17 us (2%)
    dot_general x5, matrix products, layer(): up = jnp.dot(a, w['w_up'], preferred_element_type=jnp.float32)  173 us
    dot_general x5, matrix products, layer(): gate = jnp.dot(a, w['w_gate'], preferred_element_type=jnp.float32)  165 us
    psum x1, waiting for transfers between devices, summed(): lax.psum(lax.psum_scatter(term, 's', scatter_dimension=0, tiled=True), 'r')  148 us
    dot_general x5, matrix products, matmul(): jnp.dot(a, w, preferred_element_type=jnp.float32).astype(jnp.bfloat16)  137 us
    reduce_scatter x6, waiting for transfers between devices, summed(): lax.psum_scatter(term, 's', scatter_dimension=0, tiled=True)  63.3 us
    unnamed x36, local copies, waits for them, and re-layouts  30.1 us
    all_gather x6, waiting for transfers between devices, fetched(): lax.all_gather(w[number], 's', axis=0, tiled=True)  19.9 us
    convert_element_type x2, other arithmetic, adamw(): return ((w - 0.02 * step).astype(jnp.bfloat16), m, v)  17.8 us
  transfers between devices with their start and end apart: 13, of which 7 were waited for; matrix products, arithmetic and copies ran while one was open for 46% of the time, Pallas kernels for 0%

commit v1 on v0

v1 whole, which is shorter than its diff:
```python
import functools

import jax
import jax.numpy as jnp
from jax import lax
from jax.experimental import pallas as pl
from jax.experimental.pallas import tpu as pltpu
from jax.sharding import PartitionSpec as P

NAMES = ("w_gate", "w_up", "w_down")
BF, F32 = jnp.bfloat16, jnp.float32
MESH = pl.DeviceIdType.MESH
VMEM, ANY, DMA = pltpu.VMEM, pl.ANY, pltpu.SemaphoreType.DMA

T, D, FF = 4096, 896, 2304
HALF = FF // 2
C = 256
N = FF // C
TB = 512
NT = T // TB
SLOTS = 4
GROUPS = NT // SLOTS
RB = 256


def dot(a, b, ca=1, cb=0):
    return lax.dot_general(a, b, (((ca,), (cb,)), ((), ())), preferred_element_type=F32)


def rows(i, n):
    return pl.ds(pl.multiple_of(i * n, n), n)


def norm_scale(wide):
    return lax.rsqrt(jnp.mean(wide * wide, -1, keepdims=True) + 1e-6)


def norm_in_place(ref):
    def body(i, _):
        wide = ref[rows(i, RB), :].astype(F32)
        ref[rows(i, RB), :] = (wide * norm_scale(wide)).astype(BF)
        return 0

    lax.fori_loop(0, T // RB, body, 0)


def zero(ref):
    def body(i, _):
        ref[rows(i, RB), :] = jnp.zeros((RB, D), F32)
        return 0

    lax.fori_loop(0, T // RB, body, 0)


def chunk_copies(j, slot, wg, wu, wd, bg, bu, bd, sem, which=(0, 1, 2)):
    out = []
    for half in range(2):
        at = pl.multiple_of(half * HALF + j * 128, 128)
        if 0 in which:
            out.append(pltpu.make_async_copy(wg.at[:, pl.ds(at, 128)], bg.at[slot, :, pl.ds(half * 128, 128)], sem.at[slot, half]))
        if 1 in which:
            out.append(pltpu.make_async_copy(wu.at[:, pl.ds(at, 128)], bu.at[slot, :, pl.ds(half * 128, 128)], sem.at[slot, 2 + half]))
        if 2 in which:
            out.append(pltpu.make_async_copy(wd.at[pl.ds(at, 128), :], bd.at[slot, pl.ds(half * 128, 128), :], sem.at[slot, 4 + half]))
    return out


def forward_kernel(x_ref, wg, wu, wd, h_ref, kept, a, acc, bg, bu, bd, keep, wsem, ksem, xsem):
    load = pltpu.make_async_copy(x_ref, a, xsem)
    load.start()
    weights = lambda j, slot: chunk_copies(j, slot, wg, wu, wd, bg, bu, bd, wsem)
    for copy in weights(0, 0):
        copy.start()
    load.wait()
    norm_in_place(a)
    zero(acc)

    def keep_copies(kk):
        bank = lax.rem(kk, 2)
        return [
            pltpu.make_async_copy(
                keep.at[bank, n], kept.at[kk // GROUPS, :, rows(lax.rem(kk, GROUPS) * SLOTS + n, TB), :], ksem.at[bank, n]
            )
            for n in range(SLOTS)
        ]

    def step(j, _):
        slot = lax.rem(j, 2)

        @pl.when(j + 1 < N)
        def _():
            for copy in weights(j + 1, 1 - slot):
                copy.start()

        for copy in weights(j, slot):
            copy.wait()

        def some(k, _):
            kk = j * GROUPS + k

            @pl.when(kk >= 2)
            def _():
                for copy in keep_copies(kk - 2):
                    copy.wait()

            bank = lax.rem(kk, 2)
            for n in range(SLOTS):
                s = rows(k * SLOTS + n, TB)
                at = a[s, :]
                gate, up = dot(at, bg[slot]), dot(at, bu[slot])
                keep[bank, n, 0] = gate
                keep[bank, n, 1] = up
                p = (gate * (1 / (1 + jnp.exp(-gate))) * up).astype(BF)
                acc[s, :] += dot(p, bd[slot])
            for copy in keep_copies(kk):
                copy.start()
            return 0

        lax.fori_loop(0, GROUPS, some, 0)
        return 0

    lax.fori_loop(0, N, step, 0)
    for kk in range(N * GROUPS - 2, N * GROUPS):
        for copy in keep_copies(jnp.int32(kk)):
            copy.wait()
    load.start()
    load.wait()

    def last(i, _):
        s = rows(i, RB)
        a[s, :] = (a[s, :].astype(F32) + acc[s, :].astype(BF).astype(F32)).astype(BF)
        return 0

    lax.fori_loop(0, T // RB, last, 0)
    out = pltpu.make_async_copy(a, h_ref, xsem)
    out.start()
    out.wait()


def forward(x, wg, wu, wd):
    any_ = pl.BlockSpec(memory_space=ANY)
    return pl.pallas_call(
        forward_kernel,
        in_specs=[any_] * 4,
        out_specs=[any_] * 2,
        out_shape=[jax.ShapeDtypeStruct((T, D), BF), jax.ShapeDtypeStruct((N, 2, T, C), F32)],
        scratch_shapes=[
            VMEM((T, D), BF),
            VMEM((T, D), F32),
            VMEM((2, D, C), BF),
            VMEM((2, D, C), BF),
            VMEM((2, C, D), BF),
            VMEM((2, SLOTS, 2, TB, C), F32),
            DMA((2, 6)),
            DMA((2, SLOTS)),
            DMA,
        ],
        compiler_params=pltpu.CompilerParams(vmem_limit_bytes=66_000_000),
        cost_estimate=pl.CostEstimate(flops=6 * T * D * FF, bytes_accessed=2 * T * FF * 4, transcendentals=0),
        name="forward",
    )(x, wg, wu, wd)


def backward_kernel(
    x_ref, h_ref, dy_ref, kept, wg, wu, wd, wd0,
    ggu, gd, sq_out,
    a, dy, acc, p, dg, du, bg, bu, bd, keep, res, resd,
    s1, s1d, r1, r1d, s2, s2d, own2, own2d, r2, r2d, s3, s3d, own3, own3d, r3, r3d, fin, find, sq, sqr,
    wsem, ksem, xsem, ysem, ssem, rsem, fsem, gsem, dsem, qsend, qrecv,
):
    rep, y, s_ = lax.axis_index("rep"), lax.axis_index("r"), lax.axis_index("s")
    xx, c = s_ // 2, lax.rem(s_, 2)
    at_core = (rep, y, 2 * xx + 1 - c)
    at_x = (rep, y, 2 * (1 - xx) + c)
    at_y = (rep, 1 - y, s_)
    at_diagonal = (rep, 1 - y, 2 * xx + 1 - c)
    me = y * 4 + s_

    barrier = pltpu.get_barrier_semaphore()
    for k in range(1, 8):
        other = lax.rem(me + k, 8)
        pl.semaphore_signal(barrier, inc=1, device_id=(rep, other // 4, lax.rem(other, 4)), device_id_type=MESH)

    weights = lambda j, slot: chunk_copies(j, slot, wg, wu, wd, bg, bu, bd, wsem)
    weights0 = lambda j, slot: chunk_copies(j, slot, wg, wu, wd0, bg, bu, bd, wsem, (2,))
    for copy in weights(0, 0):
        copy.start()
    load_a = pltpu.make_async_copy(h_ref, a, xsem)
    load_x = pltpu.make_async_copy(x_ref, a, xsem)
    load_dy = pltpu.make_async_copy(dy_ref, dy, ysem)
    load_a.start()
    load_dy.start()
    sq[...] = jnp.zeros_like(sq)
    zero(acc)
    load_a.wait()
    norm_in_place(a)
    load_dy.wait()
    pl.semaphore_wait(barrier, 7)

    def remote(src, dst, stage, kind, slot, device):
        return pltpu.make_async_remote_copy(
            src_ref=src, dst_ref=dst, send_sem=ssem.at[stage, kind], recv_sem=rsem.at[stage, kind, slot], device_id=device, device_id_type=MESH
        )

    def exchange1(jj):
        k = lax.rem(jj, 2)
        return remote(s1, r1.at[k], 0, 0, k, at_core), remote(s1d, r1d.at[k], 0, 1, k, at_core)

    def exchange2(jj):
        k = lax.rem(jj, 2)
        return remote(s2, r2.at[k], 1, 0, k, at_x), remote(s2d, r2d.at[k], 1, 1, k, at_x)

    def exchange3(jj):
        k = lax.rem(jj, 2)
        return remote(s3, r3.at[k], 2, 0, k, at_y), remote(s3d, r3d.at[k], 2, 1, k, at_y)

    def go(copies):
        for copy in copies:
            copy.start()

    def done(copies):
        for copy in copies:
            copy.wait()

    def part(which, owner_x, core):
        return pl.ds(pl.multiple_of((2 * owner_x + core) * 224, 32), 224) if which == 0 else pl.ds(pl.multiple_of(owner_x * 128 + core * 64, 64), 64)

    def stage1(jj):
        for q in range(2):
            for g in range(2):
                s1[q, g] = res[g, part(0, q, 1 - c), :].astype(BF)
            s1d[q] = resd[part(1, q, 1 - c), :].astype(BF)
        go(exchange1(jj))

    def stage2(jj):
        k = lax.rem(jj, 2)
        done(exchange1(jj))
        for g in range(2):
            s2[g] = (res[g, part(0, 1 - xx, c), :] + r1[k, 1 - xx, g].astype(F32)).astype(BF)
            own2[g] = res[g, part(0, xx, c), :] + r1[k, xx, g].astype(F32)
        s2d[...] = (resd[part(1, 1 - xx, c), :] + r1d[k, 1 - xx].astype(F32)).astype(BF)
        own2d[...] = resd[part(1, xx, c), :] + r1d[k, xx].astype(F32)
        go(exchange2(jj))

    def stage3(jj):
        k = lax.rem(jj, 2)
        done(exchange2(jj))
        mine, theirs = rows(y, 112), rows(1 - y, 112)
        for g in range(2):
            s3[g] = (own2[g, theirs, :] + r2[k, g, theirs, :].astype(F32)).astype(BF)
            own3[g] = own2[g, mine, :] + r2[k, g, mine, :].astype(F32)
        mine, theirs = rows(y, 32), rows(1 - y, 32)
        s3d[...] = (own2d[theirs, :] + r2d[k, theirs, :].astype(F32)).astype(BF)
        own3d[...] = own2d[mine, :] + r2d[k, mine, :].astype(F32)
        go(exchange3(jj))

    def place(jj):
        return 1 - jj // N, lax.rem(jj, N)

    def finished_gu(jj, far):
        layer, j = place(jj)
        to = ggu.at[layer, j, :, rows(y, 112), :]
        if not far:
            return pltpu.make_async_copy(fin, to, fsem.at[0])
        return pltpu.make_async_remote_copy(src_ref=fin, dst_ref=to, send_sem=fsem.at[1], recv_sem=gsem.at[jj], device_id=at_y, device_id_type=MESH)

    def down_at(jj, core, at):
        layer, j = place(jj)
        first = j * 128 + core * 64
        owner = first // 576
        return owner, gd.at[layer, pl.ds(pl.multiple_of(first - owner * 576 + at * 32, 32), 32), :]

    def finished_d(jj, kind):
        owner, to = down_at(jj, c, y)
        if kind == 3:
            return pltpu.make_async_copy(find, to, fsem.at[2])
        device = (at_core, at_y, at_diagonal)[kind]
        return pltpu.make_async_remote_copy(
            src_ref=find, dst_ref=to, send_sem=fsem.at[3 + kind], recv_sem=dsem.at[kind, jj], device_id=device, device_id_type=MESH
        )

    def sends(jj, act):
        act(finished_gu(jj, False), False)
        act(finished_gu(jj, True), True)
        owner, _ = down_at(jj, c, y)

        @pl.when(owner == c)
        def _():
            act(finished_d(jj, 3), False)
            act(finished_d(jj, 1), True)

        @pl.when(owner != c)
        def _():
            act(finished_d(jj, 0), True)
            act(finished_d(jj, 2), True)

    def start(copy, far):
        copy.start()

    def sent(copy, far):
        copy.wait_send() if far else copy.wait()

    def stage4(jj):
        k = lax.rem(jj, 2)
        done(exchange3(jj))

        @pl.when(jj > 0)
        def _():
            sends(jj - 1, sent)

        total = jnp.zeros((8, 128), F32)
        for g in range(2):
            f = (own3[g] + r3[k, g].astype(F32)).astype(BF)
            fin[g] = f
            f = f.astype(F32)
            total += jnp.sum((f * f).reshape(14, 8, 2, 128), (0, 2))
        f = (own3d[...] + r3d[k].astype(F32)).astype(BF)
        find[...] = f
        f = f.astype(F32)
        total += jnp.sum((f * f).reshape(4, 8, 7, 128), (0, 2))
        sq[...] += total
        sends(jj, start)

    def received(jj):
        finished_gu(jj, True).wait_recv()
        _, j = place(jj)

        @pl.when((2 * j + c) // N == c)
        def _():
            finished_d(jj, 1).wait_recv()

        @pl.when((2 * j + 1 - c) // N == c)
        def _():
            finished_d(jj, 0).wait_recv()
            finished_d(jj, 2).wait_recv()

    def stages(jj):
        @pl.when(jj >= 3)
        def _():
            stage4(jj - 3)

        @pl.when(jj >= 2)
        def _():
            stage3(jj - 2)

        @pl.when(jj >= 1)
        def _():
            stage2(jj - 1)

    def weight_gradients(jj):
        res[0] = dot(a[...], dg[...], 0, 0)
        res[1] = dot(a[...], du[...], 0, 0)
        resd[...] = dot(dy[...], p[...], 0, 0).T
        stage1(jj)

    def silu(gate):
        sigmoid = 1 / (1 + jnp.exp(-gate))
        return gate * sigmoid, sigmoid * (1 + gate * (1 - sigmoid))

    def step1(j, _):
        slot = lax.rem(j, 2)

        @pl.when(j + 1 < N)
        def _():
            go(weights(j + 1, 1 - slot))

        done(weights(j, slot))
        stages(j)

        def some(k, _):
            for n in range(SLOTS):
                s = rows(k * SLOTS + n, TB)
                at = a[s, :]
                gate, up = dot(at, bg[slot]), dot(at, bu[slot])
                dp = dot(dy[s, :], bd[slot], 1, 1).astype(BF).astype(F32)
                silu_, slope = silu(gate)
                p[s, :] = (silu_ * up).astype(BF)
                dgate, dup = (dp * up * slope).astype(BF), (dp * silu_).astype(BF)
                dg[s, :] = dgate
                du[s, :] = dup
                acc[s, :] += dot(dgate, bg[slot], 1, 1) + dot(dup, bu[slot], 1, 1)
            return 0

        lax.fori_loop(0, GROUPS, some, 0)
        weight_gradients(j)
        return 0

    lax.fori_loop(0, N, step1, 0)

    def kept_copies(kk):
        bank = lax.rem(kk, 2)
        return [
            pltpu.make_async_copy(
                kept.at[kk // GROUPS, :, rows(lax.rem(kk, GROUPS) * SLOTS + n, TB), :], keep.at[bank, n], ksem.at[bank, n]
            )
            for n in range(SLOTS)
        ]

    go(kept_copies(jnp.int32(0)) + kept_copies(jnp.int32(1)))
    go(weights0(0, 0))
    load_a.start()
    load_a.wait()

    def between(i, _):
        s = rows(i, RB)
        wide, da = a[s, :].astype(F32), acc[s, :].astype(BF).astype(F32)
        scale = norm_scale(wide)
        inner = jnp.mean(da * wide, -1, keepdims=True)
        back = (da * scale - wide * (scale * scale * scale * inner)).astype(BF).astype(F32)
        dy[s, :] = (dy[s, :].astype(F32) + back).astype(BF)
        return 0

    lax.fori_loop(0, T // RB, between, 0)
    load_x.start()
    load_x.wait()
    norm_in_place(a)

    def step0(j, _):
        slot = lax.rem(j, 2)

        @pl.when(j + 1 < N)
        def _():
            go(weights0(j + 1, 1 - slot))

        done(weights0(j, slot))
        stages(N + j)

        def some(k, _):
            kk = j * GROUPS + k
            bank = lax.rem(kk, 2)
            done(kept_copies(kk))
            for n in range(SLOTS):
                s = rows(k * SLOTS + n, TB)
                dp = dot(dy[s, :], bd[slot], 1, 1).astype(BF).astype(F32)
                gate, up = keep[bank, n, 0], keep[bank, n, 1]
                silu_, slope = silu(gate)
                p[s, :] = (silu_ * up).astype(BF)
                dg[s, :] = (dp * up * slope).astype(BF)
                du[s, :] = (dp * silu_).astype(BF)

            @pl.when(kk + 2 < N * GROUPS)
            def _():
                go(kept_copies(kk + 2))

            return 0

        lax.fori_loop(0, GROUPS, some, 0)
        weight_gradients(N + j)
        return 0

    lax.fori_loop(0, N, step0, 0)
    stage4(2 * N - 3)
    stage3(2 * N - 2)
    stage2(2 * N - 1)
    stage4(2 * N - 2)
    stage3(2 * N - 1)
    stage4(2 * N - 1)

    def square(k):
        other = lax.rem(me + k, 8)
        return pltpu.make_async_remote_copy(
            src_ref=sq, dst_ref=sqr.at[me], send_sem=qsend.at[k - 1], recv_sem=qrecv.at[k - 1],
            device_id=(rep, other // 4, lax.rem(other, 4)), device_id_type=MESH,
        )

    for k in range(1, 8):
        square(k).start()
    sends(2 * N - 1, sent)

    def all_received(jj, _):
        received(jj)
        return 0

    lax.fori_loop(0, 2 * N, all_received, 0)
    for k in range(1, 8):
        came_from = lax.rem(me + 8 - k, 8)
        pltpu.make_async_remote_copy(
            src_ref=sq, dst_ref=sqr.at[came_from], send_sem=qsend.at[k - 1], recv_sem=qrecv.at[k - 1],
            device_id=at_y, device_id_type=MESH,
        ).wait()
    sqr[me] = sq[...]
    sq_out[...] = functools.reduce(lambda t, k: t + sqr[k], range(1, 8), sqr[0])


def backward(x, h, dy, kept, wg, wu, wd, wd0):
    any_ = pl.BlockSpec(memory_space=ANY)
    return pl.pallas_call(
        backward_kernel,
        in_specs=[any_] * 8,
        out_specs=[any_, any_, pl.BlockSpec(memory_space=VMEM)],
        out_shape=[
            jax.ShapeDtypeStruct((2, N, 2, 224, C), BF),
            jax.ShapeDtypeStruct((2, 576, D), BF),
            jax.ShapeDtypeStruct((8, 128), F32),
        ],
        scratch_shapes=[
            VMEM((T, D), BF), VMEM((T, D), BF), VMEM((T, D), F32),
            VMEM((T, C), BF), VMEM((T, C), BF), VMEM((T, C), BF),
            VMEM((2, D, C), BF), VMEM((2, D, C), BF), VMEM((2, C, D), BF),
            VMEM((2, SLOTS, 2, TB, C), F32),
            VMEM((2, D, C), F32), VMEM((C, D), F32),
            VMEM((2, 2, 224, C), BF), VMEM((2, 64, D), BF), VMEM((2, 2, 2, 224, C), BF), VMEM((2, 2, 64, D), BF),
            VMEM((2, 224, C), BF), VMEM((64, D), BF), VMEM((2, 224, C), F32), VMEM((64, D), F32),
            VMEM((2, 2, 224, C), BF), VMEM((2, 64, D), BF),
            VMEM((2, 112, C), BF), VMEM((32, D), BF), VMEM((2, 112, C), F32), VMEM((32, D), F32),
            VMEM((2, 2, 112, C), BF), VMEM((2, 32, D), BF),
            VMEM((2, 112, C), BF), VMEM((32, D), BF), VMEM((8, 128), F32), VMEM((8, 8, 128), F32),
            DMA((2, 6)), DMA((2, SLOTS)), DMA, DMA,
            DMA((3, 2)), DMA((3, 2, 2)), DMA((6,)), DMA((2 * N,)), DMA((3, 2 * N)), DMA((7,)), DMA((7,)),
        ],
        compiler_params=pltpu.CompilerParams(vmem_limit_bytes=66_000_000, collective_id=0, has_side_effects=True),
        cost_estimate=pl.CostEstimate(flops=24 * T * D * FF, bytes_accessed=2 * T * FF * 4, transcendentals=0),
        name="backward",
    )(x, h, dy, kept, wg, wu, wd, wd0)


def adamw(w, m, v, g):
    m = 0.9 * m + 0.1 * g
    v = 0.95 * v + 0.05 * g * g
    step = m * lax.rsqrt(v + 1e-8) + 0.1 * w
    return (w - 0.02 * step).astype(jnp.bfloat16), m, v


def solution(mesh):
    def step(x, dy, *arrays):
        weights, m, v = (arrays[i : i + 3] for i in (0, 3, 6))
        whole = [[lax.all_gather(w[n], "s", axis=0, tiled=True) for w in weights] for n in range(2)]
        h, kept = forward(x[0], *whole[0])
        ggu, gd, squares = backward(x[0], h, dy[0], kept, *whole[1], whole[0][2])
        gu = ggu.reshape(2, N, 2, 224, 2, 128).transpose(2, 0, 3, 4, 1, 5).reshape(2, 2, 224, FF)
        count = 3 * 2 * D * FF
        factor = jnp.minimum(1.0, 0.5 * lax.rsqrt(jnp.sum(squares) / count + 1e-30))
        new = [adamw(w.astype(F32), m, v, g.astype(F32) * factor) for w, m, v, g in zip(weights, m, v, (gu[0], gu[1], gd), strict=True)]
        return tuple(one[which] for which in range(3) for one in new)

    states, cut = P(("rep", "r", "s"), None, None), P(None, "s", None)
    return jax.shard_map(
        step,
        mesh=mesh,
        in_specs=(states, states) + (cut,) * 9,
        out_specs=(P("rep", "s", None),) * 9,
        check_vma=False,
    )
```

time: 818 us -> 660 us (0.81)
  matrix products: 475 us -> 0 us
  Pallas kernels: 0 us -> 432 us
  waiting for transfers between devices: 233 us -> 85.3 us
  local copies, waits for them, and re-layouts: 37.7 us -> 88.7 us
  other arithmetic: 41.8 us -> 31.6 us
    dot_general x15 -> x0, matrix products: 475 us -> none  [the longest x5 173 us: layer(): up = jnp.dot(a, w['w_up'], preferred_element_type=jnp.float32)]
    pallas_call x0 -> x2, Pallas kernels: none -> 432 us  [the longest x1 352 us: backward(): pl.pallas_call(backward_kernel, in_specs=[any_] * 8, out_specs=[any_, any...]
    psum x1 -> x0, waiting for transfers between devices: 148 us -> none  [summed(): lax.psum(lax.psum_scatter(term, 's', scatter_dimension=0, tiled=True), 'r')]
    all_gather x6, waiting for transfers between devices: 19.9 us -> 83.7 us  [step(): lax.all_gather(w[n], 's', axis=0, tiled=True)]
    reduce_scatter x6 -> x0, waiting for transfers between devices: 63.3 us -> none  [summed(): lax.psum_scatter(term, 's', scatter_dimension=0, tiled=True)]
    unnamed x36 -> x24, local copies, waits for them, and re-layouts: 30.1 us -> 60 us
    reshape x0 -> x2, local copies, waits for them, and re-layouts: none -> 21.2 us  [step(): ggu.reshape(2, N, 2, 224, 2, 128).transpose(2, 0, 3, 4, 1, 5)]
    reduce_sum x4 -> x1, other arithmetic: 14.1 us -> 1.29 us  [step(): factor = jnp.minimum(1.0, 0.5 * lax.rsqrt(jnp.sum(squares) / count + 1e-30))]
  transfers between devices with their start and end apart: 13 -> 6, of which waited for: 7 -> 3; matrix products, arithmetic and copies ran while one was open for 46% -> 5% of each run, Pallas kernels for 0% -> 12%
where the time goes in v1:
time: 660 us; the launch traced here: 653 us
  Pallas kernels  432 us (65%)
  local copies, waits for them, and re-layouts  88.7 us (13%)
  waiting for transfers between devices  85.3 us (13%)
  other arithmetic  31.6 us (5%)
  between operations  15.4 us (2%)
    pallas_call x1, Pallas kernels, backward(): pl.pallas_call(backward_kernel, in_specs=[any_] * 8, out_specs=[any_, any...  352 us
    all_gather x6, waiting for transfers between devices, step(): lax.all_gather(w[n], 's', axis=0, tiled=True)  83.7 us
    pallas_call x1, Pallas kernels, forward(): pl.pallas_call(forward_kernel, in_specs=[any_] * 4, out_specs=[any_] * 2,...  80.1 us
    unnamed x24, local copies, waits for them, and re-layouts  60 us
    convert_element_type x3, other arithmetic, adamw(): return ((w - 0.02 * step).astype(jnp.bfloat16), m, v)  24.7 us
    reshape x2, local copies, waits for them, and re-layouts, step(): ggu.reshape(2, N, 2, 224, 2, 128).transpose(2, 0, 3, 4, 1, 5)  21.2 us
  transfers between devices with their start and end apart: 6, of which 3 were waited for; matrix products, arithmetic and copies ran while one was open for 5% of the time, Pallas kernels for 12%

profile of v1, /device:TPU:0, one launch (start us, length us, event | category | flops | bytes accessed | tf_op | source)
XLA Modules:
  0.0 653.3 jit_solution(6429319724395836227)
XLA Ops:
  7.2 3.1 fusion.15
  10.4 3.0 fusion.17
  16.7 2.4 copy.26
  19.1 4.1 copy.22
  23.2 5.8 copy.27
  29.1 5.8 copy.28
  34.9 5.8 copy.23
  40.7 5.9 copy.25
  46.6 31.2 %all-gather.13.cloned.1.call-done = bf16[1,896,2304]{2,1,0:T(8,128)(2,1)} async-done(((bf16[1,224,2304]{2,1,0:T(8,128)(2,1)}), bf16[1,896,2304]{2,1,0:T(8,128)(2,1)}) %all-gather.13.cloned.1.call-update) | async-done | bytes 4128784 | tf_op jit(solution)/shard_map/all_gather | solution.py:527
  77.8 33.3 %all-gather.15.cloned.1.call-done = bf16[1,896,2304]{2,1,0:T(8,128)(2,1)} async-done(((bf16[1,224,2304]{2,1,0:T(8,128)(2,1)}), bf16[1,896,2304]{2,1,0:T(8,128)(2,1)}) %all-gather.15.cloned.1.call-update) | async-done | bytes 4128784 | tf_op jit(solution)/shard_map/all_gather | solution.py:527
  111.0 80.1 %forward.1 = (bf16[4096,896]{1,0:T(8,128)(2,1)}, f32[9,2,4096,256]{3,2,1,0:T(8,128)}) custom-call(bf16[4096,896]{1,0:T(8,128)(2,1)} %bitcast.18, bf16[896,2304]{1,0:T(8,128)(2,1)} %bitcast.23, bf16[896,2304]{1,0:T(8,128)(2,1)} %bitcast.25, bf16[2304,896]{1,0:T(8,128)(2,1)} %bitcast.21), custom_call_target="tpu_custom_call" | custom-call | flops 50734301184 | bytes 75497472 | tf_op jit(solution)/shard_map/forward/pallas_call | solution.py:142
  191.2 19.2 %all-gather.23.cloned.1.call-done = bf16[1,2304,896]{2,1,0:T(8,128)(2,1)} async-done(((bf16[1,576,896]{2,1,0:T(8,128)(2,1)}), bf16[1,2304,896]{2,1,0:T(8,128)(2,1)}) %all-gather.23.cloned.1.call-update) | async-done | bytes 4128784 | tf_op jit(solution)/shard_map/all_gather | solution.py:527
  210.4 351.9 %backward.1 = (bf16[2,9,2,224,256]{4,3,2,1,0:T(8,128)(2,1)}, bf16[2,576,896]{2,1,0:T(8,128)(2,1)}, f32[8,128]{1,0:T(8,128)}) custom-call(bf16[4096,896]{1,0:T(8,128)(2,1)} %bitcast.19, bf16[4096,896]{1,0:T(8,128)(2,1)} %get-tuple-element.14.h_ref, bf16[4096,896]{1,0:T(8,128)(2,1)} %bitcast.20, f32[9,2,4096,256]{3,2,1,0:T(8,128)} %get-tuple-element.15.kept, ...), custom_call_target="tpu_custom_call" | custom-call | flops 202937204736 | bytes 75497472 | tf_op jit(solution)/shard_map/backward/pallas_call | solution.py:487
  564.3 8.7 %reshape.32 = bf16[2,9,2,224,2,128]{5,4,3,2,1,0:T(2,128)(2,1)} reshape(bf16[2,9,2,224,256]{4,3,2,1,0:T(8,128)(2,1)} %get-tuple-element.16) | data formatting | bytes 8257536 | tf_op jit(solution)/shard_map/reshape | solution.py:530
  573.0 12.5 %copy.24 = bf16[2,9,2,224,2,128]{3,5,1,4,0,2:T(8,128)(2,1)} copy(bf16[2,9,2,224,2,128]{5,4,3,2,1,0:T(2,128)(2,1)} %reshape.32) | data formatting | bytes 8257536 | tf_op jit(solution)/shard_map/reshape | solution.py:530
  585.6 5.6 convert_multiply_fusion.3
  591.2 6.7 %fusion.5 = (bf16[2,224,2304]{1,2,0:T(8,128)(2,1)}, f32[2,224,2304]{1,2,0:T(8,128)}, f32[2,224,2304]{1,2,0:T(8,128)}) fusion(bf16[2,224,2304]{1,2,0:T(8,128)(2,1)S(1)} %copy-done.1, f32[2,224,2304]{1,2,0:T(8,128)S(1)} %bitcast.16, f32[2,224,2304]{1,2,0:T(8,128)} %copy.28, f32[2,224,2304]{1,2,0:T(8,128)S(1)} %bitcast.14), kind=kLoop, calls=%fused_computation.14 | loop fusion | flops 15482880 | bytes 24772608 | tf_op jit(solution)/shard_map/convert_element_type | solution.py:521
  597.9 5.8 copy.32
  603.7 6.0 copy.34
  609.7 4.2 copy.30
  613.8 9.7 %fusion.2 = (bf16[2,224,2304]{1,2,0:T(8,128)(2,1)}, f32[2,224,2304]{1,2,0:T(8,128)}, f32[2,224,2304]{1,2,0:T(8,128)}) fusion(bf16[2,224,2304]{1,2,0:T(8,128)(2,1)S(1)} %copy-done, f32[2,224,2304]{1,2,0:T(8,128)} %bitcast.15, f32[2,224,2304]{1,2,0:T(8,128)} %copy.25, f32[2,224,2304]{1,2,0:T(8,128)} %copy.23), kind=kLoop, calls=%fused_computation.11 | loop fusion | flops 15482880 | bytes 24772608 | tf_op jit(solution)/shard_map/convert_element_type | solution.py:521
  623.6 5.8 copy.31
  629.4 6.0 copy.33
  637.7 8.3 %fusion.10 = (bf16[2,576,896]{2,1,0:T(8,128)(2,1)}, f32[2,576,896]{2,1,0:T(8,128)}, f32[2,576,896]{2,1,0:T(8,128)}) fusion(bf16[2,576,896]{2,1,0:T(8,128)(2,1)} %param.15, f32[]{:T(128)S(6)} %min_shard_map.3, bf16[2,576,896]{2,1,0:T(8,128)(2,1)} %get-tuple-element.18, f32[2,576,896]{2,1,0:T(8,128)} %param.21, f32[2,576,896]{2,1,0:T(8,128)} %param.18), kind=kLoop, calls=%fused_computation.23 | loop fusion | flops 17547264 | bytes 22708228 | tf_op jit(solution)/shard_map/convert_element_type | solution.py:521
  (31 shorter events, 7.0 us)
Async XLA Ops:
  7.2 6.3 copy-start.3
  7.2 39.4 %all-gather.17.cloned.1.call-start = ((), (), s32[]{:S(2)}) async-start(), calls=%async_computation.2 | async-start | bytes 5160960 | tf_op jit(solution)/shard_map/all_gather | solution.py:527
  10.4 67.4 %all-gather.13.cloned.1.call-start = ((), (), s32[]{:S(2)}) async-start(), calls=%async_computation | async-start | bytes 5160960 | tf_op jit(solution)/shard_map/all_gather | solution.py:527
  13.4 97.6 %all-gather.15.cloned.1.call-start = ((), (), s32[]{:S(2)}) async-start(), calls=%async_computation.1 | async-start | bytes 5160960 | tf_op jit(solution)/shard_map/all_gather | solution.py:527
  14.9 176.2 %all-gather.19.cloned.1.call-start = ((), (), s32[]{:S(2)}) async-start(), calls=%async_computation.3 | async-start | bytes 5160960 | tf_op jit(solution)/shard_map/all_gather | solution.py:527
  15.5 175.7 %all-gather.21.cloned.1.call-start = ((), (), s32[]{:S(2)}) async-start(), calls=%async_computation.4 | async-start | bytes 5160960 | tf_op jit(solution)/shard_map/all_gather | solution.py:527
  16.1 194.3 %all-gather.23.cloned.1.call-start = ((), (), s32[]{:S(2)}) async-start(), calls=%async_computation.5 | async-start | bytes 5160960 | tf_op jit(solution)/shard_map/all_gather | solution.py:527
  573.0 18.2 %slice-start = ((s8[4718592]{0:T(1024)(128)(4,1)}), s8[524288]{0:T(1024)(128)(4,1)S(1)}, s32[]{:S(2)}) async-start(s8[4718592]{0:T(1024)(128)(4,1)} %bitcast.13), calls=%async_computation.6 | async-start | bytes 1048576
  585.5 5.7 slice-start.1
  585.6 5.7 copy-start.1
  603.7 10.1 %copy-start = (bf16[2,224,2304]{1,2,0:T(8,128)(2,1)S(1)}, bf16[2,224,2304]{1,2,0:T(8,128)(2,1)}, u32[]{:S(2)}) copy-start(bf16[2,224,2304]{1,2,0:T(8,128)(2,1)} %copy.22) | copy-start | bytes 6193156
  629.4 6.0 copy-start.2
Sparse Core Ops, SparseCore 0:
  10.5 33.9 all-gather.16
  46.6 31.1 all-gather.12
  79.9 31.1 all-gather.14
  113.0 31.1 all-gather.18
  146.1 31.1 all-gather.20
  179.2 31.1 all-gather.22

commit v2 on v1

v2 whole, which is shorter than its diff:
```python
import functools

import jax
import jax.numpy as jnp
from jax import lax
from jax.experimental import pallas as pl
from jax.experimental.pallas import tpu as pltpu
from jax.sharding import PartitionSpec as P

BF, F32 = jnp.bfloat16, jnp.float32
MESH = pl.DeviceIdType.MESH
VMEM, ANY, DMA = pltpu.VMEM, pl.ANY, pltpu.SemaphoreType.DMA

T, D, FF = 4096, 896, 2304
HALF = FF // 2
DOWN = 2
C = 256
PAIR, LANES = 2, 128
ROWS, ROWS_Y = 224, 112
UNIT, UNIT_Y = 64, 32
N = FF // C
ALL = PAIR * N
TB = 512
NT = T // TB
SLOTS = 4
GROUPS = NT // SLOTS
GT = SLOTS * TB
RB = 256


def dot(a, b, ca=1, cb=0):
    return lax.dot_general(a, b, (((ca,), (cb,)), ((), ())), preferred_element_type=F32)


def odd(i):
    return lax.rem(i, PAIR)


def rows(i, n):
    return pl.ds(pl.multiple_of(i * n, n), n)


def silu(gate):
    sigmoid = 0.5 * jnp.tanh(0.5 * gate) + 0.5
    value = gate * sigmoid
    return value, sigmoid + value * (1 - sigmoid)


def norm_scale(wide):
    return lax.rsqrt(jnp.mean(wide * wide, -1, keepdims=True) + 1e-6)


def norm_in_place(ref):
    def body(i, _):
        wide = ref[rows(i, RB), :].astype(F32)
        ref[rows(i, RB), :] = (wide * norm_scale(wide)).astype(BF)
        return 0

    lax.fori_loop(0, T // RB, body, 0)


def zero(ref):
    def body(i, _):
        ref[rows(i, RB), :] = jnp.zeros((RB, D), F32)
        return 0

    lax.fori_loop(0, T // RB, body, 0)


def chunk_copies(j, slot, gu, d, bgu, bd, sem):
    out = [pltpu.make_async_copy(d.at[j], bd.at[slot], sem.at[slot, 0])]
    if gu is not None:
        out.append(pltpu.make_async_copy(gu.at[j], bgu.at[slot], sem.at[slot, 1]))
    return out


def go(copies):
    for copy in copies:
        copy.start()


def done(copies):
    for copy in copies:
        copy.wait()


def where():
    rep, y, s = lax.axis_index("rep"), lax.axis_index("r"), lax.axis_index("s")
    x, c = s // 2, odd(s)
    return x, y, c, (rep, y, 2 * x + 1 - c), (rep, y, 2 * (1 - x) + c), (rep, 1 - y, s), (rep, 1 - y, 2 * x + 1 - c)


def forward_kernel(
    x_ref, wg, wu, wd, h_ref, kept, gu1, d1, d0,
    a, acc, gu, d, keep,
    lsem, lsemd, ksem, xsem, ssem, rsem, ssemd, rsemd, osem,
):
    x, y, c, at_core, at_x, at_y, _ = where()
    barrier = pltpu.get_barrier_semaphore()
    for device in (at_core, at_x, at_y):
        pl.semaphore_signal(barrier, inc=1, device_id=device, device_id_type=MESH)

    def block(q, owner_x, core, half=None):
        first = (2 * owner_x + core) * ROWS
        n = ROWS if half is None else ROWS_Y
        if half is not None:
            first = first + half * ROWS_Y
        return gu.at[q, :, pl.ds(pl.multiple_of(first, 16), n), :]

    def block_d(q, owner_x, h, half=None):
        first = owner_x * LANES + h * UNIT
        n = UNIT if half is None else UNIT_Y
        if half is not None:
            first = first + half * UNIT_Y
        return d.at[q, pl.ds(pl.multiple_of(first, UNIT_Y), n), :]

    def own(q):
        layer, j = q // N, lax.rem(q, N)
        out = []
        for g, w in enumerate((wg, wu)):
            for side in range(PAIR):
                at = pl.multiple_of(side * HALF + j * LANES, LANES)
                to = gu.at[q, g, pl.ds(pl.multiple_of((2 * x + c) * ROWS, 16), ROWS), pl.ds(side * LANES, LANES)]
                out.append(pltpu.make_async_copy(w.at[layer, :, pl.ds(at, LANES)], to, lsem.at[q, g, side]))
        return out

    def own_d(q, h):
        layer, j = q // N, lax.rem(q, N)
        at = pl.multiple_of(j * LANES + h * UNIT - c * 576, UNIT)
        return pltpu.make_async_copy(wd.at[layer, pl.ds(at, UNIT), :], block_d(q, x, h), lsemd.at[q, h])

    def holds(q, h, core):
        return (2 * lax.rem(q, N) + h) // N == core

    def each_d(q, core, act):
        for h in range(PAIR):

            @pl.when(holds(q, h, core))
            def _(h=h):
                act(h)

    def remote(ref, kind, q, device):
        return pltpu.make_async_remote_copy(
            src_ref=ref, dst_ref=ref, send_sem=ssem.at[kind, q], recv_sem=rsem.at[kind, q], device_id=device, device_id_type=MESH
        )

    def remote_d(ref, kind, q, h, device):
        return pltpu.make_async_remote_copy(
            src_ref=ref, dst_ref=ref, send_sem=ssemd.at[kind, q, h], recv_sem=rsemd.at[kind, q, h], device_id=device, device_id_type=MESH
        )

    TO = (at_x, at_y, at_core, at_core, at_core)

    def sent(kind, q):
        ref = (block(q, x, c, y), block(q, 1 - x, c, y), block(q, x, c), block(q, 1 - x, c, y), block(q, 1 - x, c, 1 - y))[kind]
        return remote(ref, kind, q, TO[kind])

    def sent_d(kind, q, h):
        ref = (block_d(q, x, h, y), block_d(q, 1 - x, h, y), block_d(q, x, h), block_d(q, 1 - x, h, y), block_d(q, 1 - x, h, 1 - y))[kind]
        return remote_d(ref, kind, q, h, TO[kind])

    def got(kind, q):
        o = 1 - c
        ref = (block(q, 1 - x, c, y), block(q, 1 - x, c, 1 - y), block(q, x, o), block(q, 1 - x, o, y), block(q, 1 - x, o, 1 - y))[kind]
        remote(ref, kind, q, TO[kind]).wait_recv()

    def got_d(kind, q, h):
        ref = (block_d(q, 1 - x, h, y), block_d(q, 1 - x, h, 1 - y), block_d(q, x, h), block_d(q, 1 - x, h, y), block_d(q, 1 - x, h, 1 - y))[kind]
        remote_d(ref, kind, q, h, TO[kind]).wait_recv()

    def send_all(q, _):
        for copy in own(q):
            copy.wait()
        sent(0, q).start()

        def act(h):
            own_d(q, h).wait()
            sent_d(0, q, h).start()

        each_d(q, c, act)
        return 0

    def pass_x(q):
        sent(2, q).start()
        got(0, q)
        sent(1, q).start()
        sent(3, q).start()

        def act(h):
            sent_d(2, q, h).start()
            got_d(0, q, h)
            sent_d(1, q, h).start()
            sent_d(3, q, h).start()

        each_d(q, c, act)

    def pass_y(q):
        got(1, q)
        sent(4, q).start()

        def act(h):
            got_d(1, q, h)
            sent_d(4, q, h).start()

        each_d(q, c, act)

    def ready(q):
        for kind in (2, 3, 4):
            got(kind, q)

        def act(h):
            for kind in (2, 3, 4):
                got_d(kind, q, h)

        each_d(q, 1 - c, act)

    def load_own(q, _):
        go(own(q))
        each_d(q, c, lambda h: own_d(q, h).start())
        return 0

    lax.fori_loop(0, ALL, load_own, 0)
    load = pltpu.make_async_copy(x_ref, a, xsem)
    load.start()
    pl.semaphore_wait(barrier, 3)
    lax.fori_loop(0, ALL, send_all, 0)
    zero(acc)
    load.wait()
    norm_in_place(a)
    pass_x(jnp.int32(0))
    pass_y(jnp.int32(0))

    def keep_copies(kk):
        bank = odd(kk)
        return [
            pltpu.make_async_copy(
                keep.at[bank, n], kept.at[kk // GROUPS, :, rows(lax.rem(kk, GROUPS) * SLOTS + n, TB), :], ksem.at[bank, n]
            )
            for n in range(SLOTS)
        ]

    last_chunk = ALL - 1
    save_d0 = pltpu.make_async_copy(d.at[pl.ds(0, N)], d0, osem.at[0, N])

    def saves(q):
        return [pltpu.make_async_copy(whole.at[q], to.at[q - N], osem.at[i, q - N]) for i, (whole, to) in enumerate(((gu, gu1), (d, d1)))]

    def step(j, _):
        ready(j)

        def some(k, _):
            kk = j * GROUPS + k

            @pl.when(kk < last_chunk)
            def _():
                pass_x(kk + 1)

            @pl.when(kk == 1)
            def _():
                pass_y(kk)

            @pl.when(kk >= 3)
            def _():
                pass_y(kk - 1)

            @pl.when(kk >= N + 2)
            def _():
                ready(kk - 2)
                go(saves(kk - 2))

            @pl.when(kk == last_chunk)
            def _():
                save_d0.start()

            @pl.when(kk >= 2)
            def _():
                done(keep_copies(kk - 2))

            bank = odd(kk)
            for n in range(SLOTS):
                s = rows(k * SLOTS + n, TB)
                at = a[s, :]
                gate, up = dot(at, gu[j, 0]), dot(at, gu[j, 1])
                keep[bank, n, 0] = gate
                keep[bank, n, 1] = up
                p = (silu(gate)[0] * up).astype(BF)
                acc[s, :] += dot(p, d[j])
            go(keep_copies(kk))
            return 0

        lax.fori_loop(0, GROUPS, some, 0)
        return 0

    lax.fori_loop(0, N, step, 0)
    load.start()
    pass_y(jnp.int32(last_chunk))
    load.wait()

    def last(i, _):
        s = rows(i, RB)
        a[s, :] = (a[s, :].astype(F32) + acc[s, :].astype(BF).astype(F32)).astype(BF)
        return 0

    lax.fori_loop(0, T // RB, last, 0)
    out = pltpu.make_async_copy(a, h_ref, xsem)
    out.start()

    for q in (last_chunk - 1, last_chunk):
        ready(jnp.int32(q))
        go(saves(jnp.int32(q)))

    def all_sent(q, _):
        for kind in range(5):
            sent(kind, q).wait_send()

        def act(h):
            for kind in range(5):
                sent_d(kind, q, h).wait_send()

        each_d(q, c, act)
        return 0

    lax.fori_loop(0, ALL, all_sent, 0)
    for kk in range(N * GROUPS - 2, N * GROUPS):
        done(keep_copies(jnp.int32(kk)))
    done((out, save_d0))

    def all_saved(q, _):
        done(saves(q))
        return 0

    lax.fori_loop(N, ALL, all_saved, 0)


def forward(x, wg, wu, wd):
    any_ = pl.BlockSpec(memory_space=ANY)
    return pl.pallas_call(
        forward_kernel,
        in_specs=[any_] * 4,
        out_specs=[any_] * 5,
        out_shape=[
            jax.ShapeDtypeStruct((T, D), BF),
            jax.ShapeDtypeStruct((N, 2, T, C), F32),
            jax.ShapeDtypeStruct((N, 2, D, C), BF),
            jax.ShapeDtypeStruct((N, C, D), BF),
            jax.ShapeDtypeStruct((N, C, D), BF),
        ],
        scratch_shapes=[
            VMEM((T, D), BF),
            VMEM((T, D), F32),
            VMEM((ALL, 2, D, C), BF),
            VMEM((ALL, C, D), BF),
            VMEM((PAIR, SLOTS, 2, TB, C), F32),
            DMA((ALL, 2, 2)), DMA((ALL, 2)), DMA((PAIR, SLOTS)), DMA,
            DMA((5, ALL)), DMA((5, ALL)), DMA((5, ALL, 2)), DMA((5, ALL, 2)), DMA((PAIR, N + 1)),
        ],
        compiler_params=pltpu.CompilerParams(vmem_limit_bytes=66_000_000, collective_id=1, has_side_effects=True),
        cost_estimate=pl.CostEstimate(flops=6 * T * D * FF, bytes_accessed=2 * T * FF * 4, transcendentals=0),
        name="forward",
    )(x, wg, wu, wd)


def backward_kernel(
    x_ref, h_ref, dy_ref, kept, gu1, d1, d0,
    ggu, gd, sq_out,
    a, dy, acc, p0, dg0, du0, p1, dg1, du1, bgu, bd, keep, res, resd,
    s1, s1d, r1, r1d, s2, s2d, own2, own2d, r2, r2d, s3, s3d, own3, own3d, r3, r3d, fin, find, sq, sqr,
    wsem, ksem, xsem, ysem, ssem, rsem, fsem, gsem, dsem, qsend, qrecv,
):
    rep, y, s_ = lax.axis_index("rep"), lax.axis_index("r"), lax.axis_index("s")
    xx, _, c, at_core, at_x, at_y, at_diagonal = where()
    me = y * 4 + s_

    barrier = pltpu.get_barrier_semaphore()
    for k in range(1, 8):
        other = lax.rem(me + k, 8)
        pl.semaphore_signal(barrier, inc=1, device_id=(rep, other // 4, lax.rem(other, 4)), device_id_type=MESH)

    weights = lambda j, slot: chunk_copies(j, slot, gu1, d1, bgu, bd, wsem)
    weights0 = lambda j, slot: chunk_copies(j, slot, None, d0, bgu, bd, wsem)
    for copy in weights(0, 0):
        copy.start()
    load_a = pltpu.make_async_copy(h_ref, a, xsem)
    load_x = pltpu.make_async_copy(x_ref, a, xsem)
    load_dy = pltpu.make_async_copy(dy_ref, dy, ysem)
    load_a.start()
    load_dy.start()
    sq[...] = jnp.zeros_like(sq)
    zero(acc)
    load_a.wait()
    norm_in_place(a)
    load_dy.wait()
    pl.semaphore_wait(barrier, 7)

    def remote(src, dst, stage, kind, slot, device):
        return pltpu.make_async_remote_copy(
            src_ref=src, dst_ref=dst, send_sem=ssem.at[stage, kind], recv_sem=rsem.at[stage, kind, slot], device_id=device, device_id_type=MESH
        )

    def exchange1(jj):
        k = odd(jj)
        return remote(s1, r1.at[k], 0, 0, k, at_core), remote(s1d, r1d.at[k], 0, 1, k, at_core)

    def exchange2(jj):
        k = odd(jj)
        return remote(s2, r2.at[k], 1, 0, k, at_x), remote(s2d, r2d.at[k], 1, 1, k, at_x)

    def exchange3(jj):
        k = odd(jj)
        return remote(s3, r3.at[k], 2, 0, k, at_y), remote(s3d, r3d.at[k], 2, 1, k, at_y)

    def part(which, owner_x, core):
        return pl.ds(pl.multiple_of((2 * owner_x + core) * ROWS, UNIT_Y), ROWS) if which == 0 else pl.ds(pl.multiple_of(owner_x * LANES + core * UNIT, UNIT), UNIT)

    def stage1(jj):
        k = odd(jj)
        for q in range(PAIR):
            for g in range(PAIR):
                s1[q, g] = res[k, g, part(0, q, 1 - c), :].astype(BF)
            s1d[q] = resd[k, part(1, q, 1 - c), :].astype(BF)
        go(exchange1(jj))

    def stage2(jj):
        k = odd(jj)
        done(exchange1(jj))
        for g in range(PAIR):
            s2[g] = (res[k, g, part(0, 1 - xx, c), :] + r1[k, 1 - xx, g].astype(F32)).astype(BF)
            own2[g] = res[k, g, part(0, xx, c), :] + r1[k, xx, g].astype(F32)
        s2d[...] = (resd[k, part(1, 1 - xx, c), :] + r1d[k, 1 - xx].astype(F32)).astype(BF)
        own2d[...] = resd[k, part(1, xx, c), :] + r1d[k, xx].astype(F32)
        go(exchange2(jj))

    def stage3(jj):
        k = odd(jj)
        done(exchange2(jj))
        mine, theirs = rows(y, ROWS_Y), rows(1 - y, ROWS_Y)
        for g in range(PAIR):
            s3[g] = (own2[g, theirs, :] + r2[k, g, theirs, :].astype(F32)).astype(BF)
            own3[g] = own2[g, mine, :] + r2[k, g, mine, :].astype(F32)
        mine, theirs = rows(y, UNIT_Y), rows(1 - y, UNIT_Y)
        s3d[...] = (own2d[theirs, :] + r2d[k, theirs, :].astype(F32)).astype(BF)
        own3d[...] = own2d[mine, :] + r2d[k, mine, :].astype(F32)
        go(exchange3(jj))

    def place(jj):
        return 1 - jj // N, lax.rem(jj, N)

    def finished_gu(jj, far):
        layer, j = place(jj)
        to = ggu.at[layer, j, :, rows(y, ROWS_Y), :]
        if not far:
            return pltpu.make_async_copy(fin, to, fsem.at[0])
        return pltpu.make_async_remote_copy(src_ref=fin, dst_ref=to, send_sem=fsem.at[1], recv_sem=gsem.at[jj], device_id=at_y, device_id_type=MESH)

    def down_at(jj, core, at):
        layer, j = place(jj)
        first = j * LANES + core * UNIT
        owner = first // 576
        return owner, gd.at[layer, pl.ds(pl.multiple_of(first - owner * 576 + at * UNIT_Y, UNIT_Y), UNIT_Y), :]

    def finished_d(jj, kind):
        owner, to = down_at(jj, c, y)
        if kind == 3:
            return pltpu.make_async_copy(find, to, fsem.at[2])
        device = (at_core, at_y, at_diagonal)[kind]
        return pltpu.make_async_remote_copy(
            src_ref=find, dst_ref=to, send_sem=fsem.at[3 + kind], recv_sem=dsem.at[kind, jj], device_id=device, device_id_type=MESH
        )

    def sends(jj, act):
        act(finished_gu(jj, False), False)
        act(finished_gu(jj, True), True)
        owner, _ = down_at(jj, c, y)

        @pl.when(owner == c)
        def _():
            act(finished_d(jj, 3), False)
            act(finished_d(jj, 1), True)

        @pl.when(owner != c)
        def _():
            act(finished_d(jj, 0), True)
            act(finished_d(jj, 2), True)

    def start(copy, far):
        copy.start()

    def sent(copy, far):
        copy.wait_send() if far else copy.wait()

    def stage4(jj):
        k = odd(jj)
        done(exchange3(jj))

        @pl.when(jj > 0)
        def _():
            sends(jj - 1, sent)

        total = jnp.zeros((8, LANES), F32)
        for g in range(PAIR):
            f = (own3[g] + r3[k, g].astype(F32)).astype(BF)
            fin[g] = f
            f = f.astype(F32)
            total += jnp.sum((f * f).reshape(14, 8, 2, LANES), (0, 2))
        f = (own3d[...] + r3d[k].astype(F32)).astype(BF)
        find[...] = f
        f = f.astype(F32)
        total += jnp.sum((f * f).reshape(4, 8, 7, LANES), (0, 2))
        sq[...] += total
        sends(jj, start)

    def received(jj):
        finished_gu(jj, True).wait_recv()
        _, j = place(jj)

        @pl.when((2 * j + c) // N == c)
        def _():
            finished_d(jj, 1).wait_recv()

        @pl.when((2 * j + 1 - c) // N == c)
        def _():
            finished_d(jj, 0).wait_recv()
            finished_d(jj, 2).wait_recv()

    def stages(jj):
        for back, stage in ((4, stage4), (3, stage3), (2, stage2), (1, stage1)):

            @pl.when(jj >= back)
            def _(back=back, stage=stage):
                stage(jj - back)

    banks = ((dg0, du0, p0), (dg1, du1, p1))

    def gradient(which, group, slot):
        left = (dy if which == DOWN else a)[pl.ds(group * GT, GT), :]
        term = dot(left, banks[group][which][...], 0, 0)
        if which == DOWN:
            term = term.T
            resd[slot] = term if group == 0 else resd[slot] + term
        else:
            res[slot, which] = term if group == 0 else res[slot, which] + term

    def clear():
        for ref in banks[1]:
            ref[...] = jnp.zeros((GT, C), BF)

    clear()

    def step1(j, _):
        slot = odd(j)

        @pl.when(j + 1 < N)
        def _():
            go(weights(j + 1, 1 - slot))

        done(weights(j, slot))

        for group in range(GROUPS):
            dg, du, p = banks[group]
            for n in range(SLOTS):
                s, b = pl.ds((group * SLOTS + n) * TB, TB), pl.ds(n * TB, TB)
                at = a[s, :]
                gate, up = dot(at, bgu[slot, 0]), dot(at, bgu[slot, 1])
                dp = dot(dy[s, :], bd[slot], 1, 1).astype(BF).astype(F32)
                if n < 3:
                    gradient(n, 1 - group, slot if group else 1 - slot)
                silu_, slope = silu(gate)
                p[b, :] = (silu_ * up).astype(BF)
                dgate, dup = (dp * up * slope).astype(BF), (dp * silu_).astype(BF)
                dg[b, :] = dgate
                du[b, :] = dup
                acc[s, :] += dot(dgate, bgu[slot, 0], 1, 1) + dot(dup, bgu[slot, 1], 1, 1)
            if group == 0:
                stages(j)
        return 0

    lax.fori_loop(0, N, step1, 0)

    def kept_copies(j, group):
        return [
            pltpu.make_async_copy(kept.at[j, :, pl.ds((group * SLOTS + n) * TB, TB), :], keep.at[group, n], ksem.at[group, n])
            for n in range(SLOTS)
        ]

    go(kept_copies(0, 0) + kept_copies(0, 1))
    for which in range(3):
        gradient(which, 1, (N - 1) % 2)
    clear()
    go(weights0(0, 0))
    load_a.start()
    load_a.wait()

    def between(i, _):
        s = rows(i, RB)
        wide, da = a[s, :].astype(F32), acc[s, :].astype(BF).astype(F32)
        scale = norm_scale(wide)
        inner = jnp.mean(da * wide, -1, keepdims=True)
        back = (da * scale - wide * (scale * scale * scale * inner)).astype(BF).astype(F32)
        dy[s, :] = (dy[s, :].astype(F32) + back).astype(BF)
        return 0

    lax.fori_loop(0, T // RB, between, 0)
    load_x.start()
    load_x.wait()
    norm_in_place(a)

    def step0(j, _):
        slot = odd(j)

        @pl.when(j + 1 < N)
        def _():
            go(weights0(j + 1, 1 - slot))

        done(weights0(j, slot))
        out = lax.rem(N + j, 2)
        for group in range(GROUPS):
            dg, du, p = banks[group]
            done(kept_copies(j, group))
            for n in range(SLOTS):
                s, b = pl.ds((group * SLOTS + n) * TB, TB), pl.ds(n * TB, TB)
                dp = dot(dy[s, :], bd[slot], 1, 1).astype(BF).astype(F32)
                if n < 3:
                    gradient(n, 1 - group, out if group else 1 - out)
                gate, up = keep[group, n, 0], keep[group, n, 1]
                silu_, slope = silu(gate)
                p[b, :] = (silu_ * up).astype(BF)
                dg[b, :] = (dp * up * slope).astype(BF)
                du[b, :] = (dp * silu_).astype(BF)

            @pl.when(j + 1 < N)
            def _(group=group):
                go(kept_copies(j + 1, group))

            if group == 0:
                stages(N + j)
        return 0

    lax.fori_loop(0, N, step0, 0)
    for which in range(3):
        gradient(which, 1, 1)
    end = jnp.int32(ALL - 1)
    stage4(end - 3)
    stage3(end - 2)
    stage2(end - 1)
    stage1(end)
    stage4(end - 2)
    stage3(end - 1)
    stage2(end)
    stage4(end - 1)
    stage3(end)
    stage4(end)

    def square(k):
        other = lax.rem(me + k, 8)
        return pltpu.make_async_remote_copy(
            src_ref=sq, dst_ref=sqr.at[me], send_sem=qsend.at[k - 1], recv_sem=qrecv.at[k - 1],
            device_id=(rep, other // 4, lax.rem(other, 4)), device_id_type=MESH,
        )

    for k in range(1, 8):
        square(k).start()
    sends(end, sent)

    def all_received(jj, _):
        received(jj)
        return 0

    lax.fori_loop(0, ALL, all_received, 0)
    for k in range(1, 8):
        came_from = lax.rem(me + 8 - k, 8)
        pltpu.make_async_remote_copy(
            src_ref=sq, dst_ref=sqr.at[came_from], send_sem=qsend.at[k - 1], recv_sem=qrecv.at[k - 1],
            device_id=at_y, device_id_type=MESH,
        ).wait()
    sqr[me] = sq[...]
    sq_out[...] = functools.reduce(lambda t, k: t + sqr[k], range(1, 8), sqr[0])


def backward(x, h, dy, kept, gu1, d1, d0):
    any_ = pl.BlockSpec(memory_space=ANY)
    return pl.pallas_call(
        backward_kernel,
        in_specs=[any_] * 7,
        out_specs=[any_, any_, pl.BlockSpec(memory_space=VMEM)],
        out_shape=[
            jax.ShapeDtypeStruct((2, N, 2, ROWS, C), BF),
            jax.ShapeDtypeStruct((2, 576, D), BF),
            jax.ShapeDtypeStruct((8, LANES), F32),
        ],
        scratch_shapes=[
            VMEM((T, D), BF), VMEM((T, D), BF), VMEM((T, D), F32),
            *[VMEM((GT, C), BF)] * 6,
            VMEM((PAIR, 2, D, C), BF), VMEM((PAIR, C, D), BF),
            VMEM((PAIR, SLOTS, 2, TB, C), F32),
            VMEM((PAIR, 2, D, C), F32), VMEM((PAIR, C, D), F32),
            VMEM((PAIR, 2, ROWS, C), BF), VMEM((PAIR, UNIT, D), BF), VMEM((PAIR, 2, 2, ROWS, C), BF), VMEM((PAIR, 2, UNIT, D), BF),
            VMEM((PAIR, ROWS, C), BF), VMEM((UNIT, D), BF), VMEM((PAIR, ROWS, C), F32), VMEM((UNIT, D), F32),
            VMEM((PAIR, 2, ROWS, C), BF), VMEM((PAIR, UNIT, D), BF),
            VMEM((PAIR, ROWS_Y, C), BF), VMEM((UNIT_Y, D), BF), VMEM((PAIR, ROWS_Y, C), F32), VMEM((UNIT_Y, D), F32),
            VMEM((PAIR, 2, ROWS_Y, C), BF), VMEM((PAIR, UNIT_Y, D), BF),
            VMEM((PAIR, ROWS_Y, C), BF), VMEM((UNIT_Y, D), BF), VMEM((8, LANES), F32), VMEM((8, 8, LANES), F32),
            DMA((PAIR, 2)), DMA((PAIR, SLOTS)), DMA, DMA,
            DMA((3, 2)), DMA((3, 2, 2)), DMA((6,)), DMA((ALL,)), DMA((3, ALL)), DMA((7,)), DMA((7,)),
        ],
        compiler_params=pltpu.CompilerParams(vmem_limit_bytes=66_000_000, collective_id=0, has_side_effects=True),
        cost_estimate=pl.CostEstimate(flops=24 * T * D * FF, bytes_accessed=2 * T * FF * 4, transcendentals=0),
        name="backward",
    )(x, h, dy, kept, gu1, d1, d0)


def adamw(w, m, v, g):
    m = 0.9 * m + 0.1 * g
    v = 0.95 * v + 0.05 * g * g
    step = m * lax.rsqrt(v + 1e-8) + 0.1 * w
    return (w - 0.02 * step).astype(jnp.bfloat16), m, v


def update_kernel(sq, *refs):
    (wg, wu, wd, mg, mu, md, vg, vu, vd, g0, g1, u0, u1, gd), out = refs[:14], refs[14:]
    mean = jnp.sum(sq[...], keepdims=True) / (3 * 2 * D * FF)
    factor = jnp.minimum(1.0, 0.5 * lax.rsqrt(mean + 1e-30))
    for i, (w, m, v, parts) in enumerate(((wg, mg, vg, (g0, g1)), (wu, mu, vu, (u0, u1)), (wd, md, vd, (gd,)))):
        width = w.shape[-1] // len(parts)
        for n, g in enumerate(parts):
            at = pl.ds(n * width, width)
            new = adamw(w[0, :, at].astype(F32), m[0, :, at], v[0, :, at], g[...].reshape(w.shape[1], width).astype(F32) * factor)
            for which in range(3):
                out[3 * which + i][0, :, at] = new[which]


def update(squares, weights, m, v, ggu, gd):
    wide = pl.BlockSpec((1, ROWS, C), lambda l, q: (l, 0, q))
    tall = pl.BlockSpec((1, 576 // N, D), lambda l, q: (l, q, 0))
    g = lambda which, n: pl.BlockSpec((1, 1, 1, ROWS, LANES), lambda l, q: (l, lax.rem(2 * q + n, N), which, 0, (2 * q + n) // N))
    return pl.pallas_call(
        update_kernel,
        grid=(2, N),
        in_specs=[pl.BlockSpec((8, LANES), lambda l, q: (0, 0))] + [wide, wide, tall] * 3 + [g(0, 0), g(0, 1), g(1, 0), g(1, 1), tall],
        out_specs=[wide, wide, tall] * 3,
        out_shape=[jax.ShapeDtypeStruct(w.shape, t) for t in (BF, F32, F32) for w in weights],
        compiler_params=pltpu.CompilerParams(vmem_limit_bytes=60_000_000),
        name="update",
    )(squares, *weights, *m, *v, ggu, ggu, ggu, ggu, gd)


def solution(mesh):
    def step(x, dy, *arrays):
        weights, m, v = (arrays[i : i + 3] for i in (0, 3, 6))
        h, kept, gu1, d1, d0 = forward(x[0], *weights)
        ggu, gd, squares = backward(x[0], h, dy[0], kept, gu1, d1, d0)
        return tuple(update(squares, weights, m, v, ggu, gd))

    states, cut = P(("rep", "r", "s"), None, None), P(None, "s", None)
    return jax.shard_map(
        step,
        mesh=mesh,
        in_specs=(states, states) + (cut,) * 9,
        out_specs=(P("rep", "s", None),) * 9,
        check_vma=False,
    )
```

time: 660 us -> 457 us (0.69)
  local copies, waits for them, and re-layouts: 88.7 us -> 0 us
  waiting for transfers between devices: 85.3 us -> 0 us
  other arithmetic: 31.6 us -> 0 us
  Pallas kernels: 432 us -> 451 us
  between operations: 15.4 us -> 1.12 us
    all_gather x6 -> x0, waiting for transfers between devices: 83.7 us -> none  [step(): lax.all_gather(w[n], 's', axis=0, tiled=True)]
    unnamed x24 -> x0, local copies, waits for them, and re-layouts: 60 us -> none
    convert_element_type x3 -> x0, other arithmetic: 24.7 us -> none  [adamw(): return ((w - 0.02 * step).astype(jnp.bfloat16), m, v)]
    reshape x2 -> x0, local copies, waits for them, and re-layouts: 21.2 us -> none  [step(): ggu.reshape(2, N, 2, 224, 2, 128).transpose(2, 0, 3, 4, 1, 5)]
    pallas_call x2 -> x3, Pallas kernels: 432 us -> 451 us  [the longest x1 322 us: backward(): pl.pallas_call(backward_kernel, in_specs=[any_] * 7, out_specs=[any_, any...]
    slice x3 -> x0, local copies, waits for them, and re-layouts: 7.53 us -> none  [step(): w[n]]
  transfers between devices with their start and end apart: 6 -> 0, of which waited for: 3 -> 0; matrix products, arithmetic and copies ran while one was open for 5% -> 0% of each run, Pallas kernels for 12% -> 0%
where the time goes in v2:
time: 457 us; the launch traced here: 452 us
  Pallas kernels  451 us (99%)
    pallas_call x1, Pallas kernels, backward(): pl.pallas_call(backward_kernel, in_specs=[any_] * 7, out_specs=[any_, any...  322 us
    pallas_call x1, Pallas kernels, forward(): pl.pallas_call(forward_kernel, in_specs=[any_] * 4, out_specs=[any_] * 5,...  101 us
    pallas_call x1, Pallas kernels, update(): pl.pallas_call(update_kernel, grid=(2, N), in_specs=[pl.BlockSpec((8, LAN...  28.6 us

profile of v2, /device:TPU:0, one launch (start us, length us, event | category | flops | bytes accessed | tf_op | source)
XLA Modules:
  0.0 452.5 jit_solution(16321669506017330595)
XLA Ops:
  0.6 100.8 %forward.1 = (bf16[4096,896]{1,0:T(8,128)(2,1)}, f32[9,2,4096,256]{3,2,1,0:T(8,128)}, bf16[9,2,896,256]{3,2,1,0:T(8,128)(2,1)}, bf16[9,256,896]{2,1,0:T(8,128)(2,1)}, bf16[9,256,896]{2,1,0:T(8,128)(2,1)}) custom-call(bf16[4096,896]{1,0:T(8,128)(2,1)} %bitcast.2, bf16[2,224,2304]{2,1,0:T(8,128)(2,1)} %refs_0_.1, bf16[2,224,2304]{2,1,0:T(8,128)(2,1)} %refs_1_.1, ...), custom_call_target="tpu_custom_call" | custom-call | flops 50734301184 | bytes 75497472 | tf_op jit(solution)/shard_map/forward/pallas_call | solution.py:337
  101.4 321.9 %backward.1 = (bf16[2,9,2,224,256]{4,3,2,1,0:T(8,128)(2,1)}, bf16[2,576,896]{2,1,0:T(8,128)(2,1)}, f32[8,128]{1,0:T(8,128)}) custom-call(bf16[4096,896]{1,0:T(8,128)(2,1)} %bitcast.3, bf16[4096,896]{1,0:T(8,128)(2,1)} %get-tuple-element.17.h_ref, bf16[4096,896]{1,0:T(8,128)(2,1)} %bitcast.4, f32[9,2,4096,256]{3,2,1,0:T(8,128)} %get-tuple-element.18.kept, ...), custom_call_target="tpu_custom_call" | custom-call | flops 202937204736 | bytes 75497472 | tf_op jit(solution)/shard_map/backward/pallas_call | solution.py:681
  423.4 28.6 %update.1 = (bf16[2,224,2304]{2,1,0:T(8,128)(2,1)}, bf16[2,224,2304]{2,1,0:T(8,128)(2,1)}, bf16[2,576,896]{2,1,0:T(8,128)(2,1)}, f32[2,224,2304]{2,1,0:T(8,128)}...) custom-call(f32[8,128]{1,0:T(8,128)} %get-tuple-element.22.sq, ...), custom_call_target="tpu_custom_call" | custom-call | tf_op jit(solution)/shard_map/update/pallas_call | solution.py:735

commit v3 on v2

--- a/solution.py
+++ b/solution.py
@@ -26,6 +26,7 @@
 GROUPS = NT // SLOTS
 GT = SLOTS * TB
 RB = 256
+EB = 512
 
 
 def dot(a, b, ca=1, cb=0):
@@ -91,9 +92,9 @@
 
 
 def forward_kernel(
-    x_ref, wg, wu, wd, h_ref, kept, gu1, d1, d0,
-    a, acc, gu, d, keep,
-    lsem, lsemd, ksem, xsem, ssem, rsem, ssemd, rsemd, osem,
+    x_ref, wg, wu, wd, h_ref, a0_ref, a1_ref, kept, gu1, d1, d0,
+    a, acc, gu, d, keep, hb, ab,
+    lsem, lsemd, ksem, xsem, ssem, rsem, ssemd, rsemd, osem, hsem,
 ):
     x, y, c, at_core, at_x, at_y, _ = where()
     barrier = pltpu.get_barrier_semaphore()
@@ -227,6 +228,8 @@
     zero(acc)
     load.wait()
     norm_in_place(a)
+    save_a0 = pltpu.make_async_copy(a, a0_ref, osem.at[1, N])
+    save_a0.start()
     pass_x(jnp.int32(0))
     pass_y(jnp.int32(0))
 
@@ -291,19 +294,30 @@
         lax.fori_loop(0, GROUPS, some, 0)
         return 0
 
+    save_a0.wait()
     lax.fori_loop(0, N, step, 0)
     load.start()
     pass_y(jnp.int32(last_chunk))
     load.wait()
 
+    def outs(i):
+        k, s = odd(i), rows(i, EB)
+        return pltpu.make_async_copy(hb.at[k], h_ref.at[s, :], hsem.at[0, k]), pltpu.make_async_copy(ab.at[k], a1_ref.at[s, :], hsem.at[1, k])
+
     def last(i, _):
-        s = rows(i, RB)
-        a[s, :] = (a[s, :].astype(F32) + acc[s, :].astype(BF).astype(F32)).astype(BF)
-        return 0
-
-    lax.fori_loop(0, T // RB, last, 0)
-    out = pltpu.make_async_copy(a, h_ref, xsem)
-    out.start()
+        @pl.when(i >= PAIR)
+        def _():
+            done(outs(i - PAIR))
+
+        k, s = odd(i), rows(i, EB)
+        h = (a[s, :].astype(F32) + acc[s, :].astype(BF).astype(F32)).astype(BF)
+        hb[k] = h
+        wide = h.astype(F32)
+        ab[k] = (wide * norm_scale(wide)).astype(BF)
+        go(outs(i))
+        return 0
+
+    lax.fori_loop(0, T // EB, last, 0)
 
     for q in (last_chunk - 1, last_chunk):
         ready(jnp.int32(q))
@@ -323,7 +337,9 @@
     lax.fori_loop(0, ALL, all_sent, 0)
     for kk in range(N * GROUPS - 2, N * GROUPS):
         done(keep_copies(jnp.int32(kk)))
-    done((out, save_d0))
+    save_d0.wait()
+    for k in range(PAIR):
+        done(outs(jnp.int32(T // EB - PAIR + k)))
 
     def all_saved(q, _):
         done(saves(q))
@@ -337,9 +353,9 @@
     return pl.pallas_call(
         forward_kernel,
         in_specs=[any_] * 4,
-        out_specs=[any_] * 5,
+        out_specs=[any_] * 7,
         out_shape=[
-            jax.ShapeDtypeStruct((T, D), BF),
+            *[jax.ShapeDtypeStruct((T, D), BF)] * 3,
             jax.ShapeDtypeStruct((N, 2, T, C), F32),
             jax.ShapeDtypeStruct((N, 2, D, C), BF),
             jax.ShapeDtypeStruct((N, C, D), BF),
@@ -351,8 +367,9 @@
             VMEM((ALL, 2, D, C), BF),
             VMEM((ALL, C, D), BF),
             VMEM((PAIR, SLOTS, 2, TB, C), F32),
+            *[VMEM((PAIR, EB, D), BF)] * 2,
             DMA((ALL, 2, 2)), DMA((ALL, 2)), DMA((PAIR, SLOTS)), DMA,
-            DMA((5, ALL)), DMA((5, ALL)), DMA((5, ALL, 2)), DMA((5, ALL, 2)), DMA((PAIR, N + 1)),
+            DMA((5, ALL)), DMA((5, ALL)), DMA((5, ALL, 2)), DMA((5, ALL, 2)), DMA((PAIR, N + 1)), DMA((PAIR, PAIR)),
         ],
         compiler_params=pltpu.CompilerParams(vmem_limit_bytes=66_000_000, collective_id=1, has_side_effects=True),
         cost_estimate=pl.CostEstimate(flops=6 * T * D * FF, bytes_accessed=2 * T * FF * 4, transcendentals=0),
@@ -361,11 +378,11 @@
 
 
 def backward_kernel(
-    x_ref, h_ref, dy_ref, kept, gu1, d1, d0,
+    h_ref, a0_ref, a1_ref, dy_ref, kept, gu1, d1, d0,
     ggu, gd, sq_out,
-    a, dy, acc, p0, dg0, du0, p1, dg1, du1, bgu, bd, keep, res, resd,
+    a, dy, acc, terms, bgu, bd, keep, hb, res, resd,
     s1, s1d, r1, r1d, s2, s2d, own2, own2d, r2, r2d, s3, s3d, own3, own3d, r3, r3d, fin, find, sq, sqr,
-    wsem, ksem, xsem, ysem, ssem, rsem, fsem, gsem, dsem, qsend, qrecv,
+    wsem, ksem, hsem, xsem, ysem, ssem, rsem, fsem, gsem, dsem, qsend, qrecv,
 ):
     rep, y, s_ = lax.axis_index("rep"), lax.axis_index("r"), lax.axis_index("s")
     xx, _, c, at_core, at_x, at_y, at_diagonal = where()
@@ -380,15 +397,14 @@
     weights0 = lambda j, slot: chunk_copies(j, slot, None, d0, bgu, bd, wsem)
     for copy in weights(0, 0):
         copy.start()
-    load_a = pltpu.make_async_copy(h_ref, a, xsem)
-    load_x = pltpu.make_async_copy(x_ref, a, xsem)
+    load_a = pltpu.make_async_copy(a1_ref, a, xsem)
+    load_a0 = pltpu.make_async_copy(a0_ref, a, xsem)
     load_dy = pltpu.make_async_copy(dy_ref, dy, ysem)
     load_a.start()
     load_dy.start()
     sq[...] = jnp.zeros_like(sq)
     zero(acc)
     load_a.wait()
-    norm_in_place(a)
     load_dy.wait()
     pl.semaphore_wait(barrier, 7)
 
@@ -529,20 +545,22 @@
             def _(back=back, stage=stage):
                 stage(jj - back)
 
-    banks = ((dg0, du0, p0), (dg1, du1, p1))
-
     def gradient(which, group, slot):
-        left = (dy if which == DOWN else a)[pl.ds(group * GT, GT), :]
-        term = dot(left, banks[group][which][...], 0, 0)
+        left = (dy if which == DOWN else a)[rows(group, GT), :]
+        term = dot(left, terms[group, which], 0, 0)
+        later = group != 0
         if which == DOWN:
-            term = term.T
-            resd[slot] = term if group == 0 else resd[slot] + term
+            resd[slot] = jnp.where(later, resd[slot], 0.0) + term.T
         else:
-            res[slot, which] = term if group == 0 else res[slot, which] + term
+            res[slot, which] = jnp.where(later, res[slot, which], 0.0) + term
+
+    def last_gradients(slot):
+        for which in (DOWN, 0, 1):
+            gradient(which, jnp.int32(1), slot)
 
     def clear():
-        for ref in banks[1]:
-            ref[...] = jnp.zeros((GT, C), BF)
+        for which in range(3):
+            terms[1, which] = jnp.zeros((GT, C), BF)
 
     clear()
 
@@ -555,54 +573,65 @@
 
         done(weights(j, slot))
 
-        for group in range(GROUPS):
-            dg, du, p = banks[group]
+        def some(group, _):
             for n in range(SLOTS):
-                s, b = pl.ds((group * SLOTS + n) * TB, TB), pl.ds(n * TB, TB)
+                s, b = rows(group * SLOTS + n, TB), pl.ds(n * TB, TB)
                 at = a[s, :]
                 gate, up = dot(at, bgu[slot, 0]), dot(at, bgu[slot, 1])
                 dp = dot(dy[s, :], bd[slot], 1, 1).astype(BF).astype(F32)
                 if n < 3:
-                    gradient(n, 1 - group, slot if group else 1 - slot)
+                    gradient(n, 1 - group, odd(slot + 1 + group))
                 silu_, slope = silu(gate)
-                p[b, :] = (silu_ * up).astype(BF)
+                terms[group, 2, b, :] = (silu_ * up).astype(BF)
                 dgate, dup = (dp * up * slope).astype(BF), (dp * silu_).astype(BF)
-                dg[b, :] = dgate
-                du[b, :] = dup
+                terms[group, 0, b, :] = dgate
+                terms[group, 1, b, :] = dup
                 acc[s, :] += dot(dgate, bgu[slot, 0], 1, 1) + dot(dup, bgu[slot, 1], 1, 1)
-            if group == 0:
+
+            @pl.when(group == 0)
+            def _():
                 stages(j)
+
+            return 0
+
+        lax.fori_loop(0, GROUPS, some, 0)
         return 0
 
     lax.fori_loop(0, N, step1, 0)
 
     def kept_copies(j, group):
         return [
-            pltpu.make_async_copy(kept.at[j, :, pl.ds((group * SLOTS + n) * TB, TB), :], keep.at[group, n], ksem.at[group, n])
+            pltpu.make_async_copy(kept.at[j, :, rows(group * SLOTS + n, TB), :], keep.at[group, n], ksem.at[group, n])
             for n in range(SLOTS)
         ]
 
-    go(kept_copies(0, 0) + kept_copies(0, 1))
-    for which in range(3):
-        gradient(which, 1, (N - 1) % 2)
+    def h_copy(i):
+        k = odd(i)
+        return pltpu.make_async_copy(h_ref.at[rows(i, EB), :], hb.at[k], hsem.at[k])
+
+    go([h_copy(jnp.int32(k)) for k in range(PAIR)] + kept_copies(0, 0) + kept_copies(0, 1))
+    last_gradients((N - 1) % 2)
+    load_a0.start()
     clear()
     go(weights0(0, 0))
-    load_a.start()
-    load_a.wait()
 
     def between(i, _):
-        s = rows(i, RB)
-        wide, da = a[s, :].astype(F32), acc[s, :].astype(BF).astype(F32)
+        k, s = odd(i), rows(i, EB)
+        h_copy(i).wait()
+        wide, da = hb[k].astype(F32), acc[s, :].astype(BF).astype(F32)
         scale = norm_scale(wide)
         inner = jnp.mean(da * wide, -1, keepdims=True)
         back = (da * scale - wide * (scale * scale * scale * inner)).astype(BF).astype(F32)
         dy[s, :] = (dy[s, :].astype(F32) + back).astype(BF)
-        return 0
-
-    lax.fori_loop(0, T // RB, between, 0)
-    load_x.start()
-    load_x.wait()
-    norm_in_place(a)
+
+        @pl.when(i + PAIR < T // EB)
+        def _():
+            h_copy(i + PAIR).start()
+
+        return 0
+
+    lax.fori_loop(0, T // EB, between, 0)
+    load_a0.wait()
 
     def step0(j, _):
         slot = odd(j)
@@ -613,31 +642,34 @@
 
         done(weights0(j, slot))
         out = lax.rem(N + j, 2)
-        for group in range(GROUPS):
-            dg, du, p = banks[group]
+        def some(group, _):
             done(kept_copies(j, group))
             for n in range(SLOTS):
-                s, b = pl.ds((group * SLOTS + n) * TB, TB), pl.ds(n * TB, TB)
+                s, b = rows(group * SLOTS + n, TB), pl.ds(n * TB, TB)
                 dp = dot(dy[s, :], bd[slot], 1, 1).astype(BF).astype(F32)
                 if n < 3:
-                    gradient(n, 1 - group, out if group else 1 - out)
+                    gradient(n, 1 - group, odd(out + 1 + group))
                 gate, up = keep[group, n, 0], keep[group, n, 1]
                 silu_, slope = silu(gate)
-                p[b, :] = (silu_ * up).astype(BF)
-                dg[b, :] = (dp * up * slope).astype(BF)
-                du[b, :] = (dp * silu_).astype(BF)
+                terms[group, 2, b, :] = (silu_ * up).astype(BF)
+                terms[group, 0, b, :] = (dp * up * slope).astype(BF)
+                terms[group, 1, b, :] = (dp * silu_).astype(BF)
 
             @pl.when(j + 1 < N)
-            def _(group=group):
+            def _():
                 go(kept_copies(j + 1, group))
 
-            if group == 0:
+            @pl.when(group == 0)
+            def _():
                 stages(N + j)
+
+            return 0
+
+        lax.fori_loop(0, GROUPS, some, 0)
         return 0
 
     lax.fori_loop(0, N, step0, 0)
-    for which in range(3):
-        gradient(which, 1, 1)
+    last_gradients(1)
     end = jnp.int32(ALL - 1)
     stage4(end - 3)
     stage3(end - 2)
@@ -676,11 +708,11 @@
     sq_out[...] = functools.reduce(lambda t, k: t + sqr[k], range(1, 8), sqr[0])
 
 
-def backward(x, h, dy, kept, gu1, d1, d0):
+def backward(h, a0, a1, dy, kept, gu1, d1, d0):
     any_ = pl.BlockSpec(memory_space=ANY)
     return pl.pallas_call(
         backward_kernel,
-        in_specs=[any_] * 7,
+        in_specs=[any_] * 8,
         out_specs=[any_, any_, pl.BlockSpec(memory_space=VMEM)],
         out_shape=[
             jax.ShapeDtypeStruct((2, N, 2, ROWS, C), BF),
@@ -689,9 +721,10 @@
         ],
         scratch_shapes=[
             VMEM((T, D), BF), VMEM((T, D), BF), VMEM((T, D), F32),
-            *[VMEM((GT, C), BF)] * 6,
+            VMEM((GROUPS, 3, GT, C), BF),
             VMEM((PAIR, 2, D, C), BF), VMEM((PAIR, C, D), BF),
             VMEM((PAIR, SLOTS, 2, TB, C), F32),
+            VMEM((PAIR, EB, D), BF),
             VMEM((PAIR, 2, D, C), F32), VMEM((PAIR, C, D), F32),
             VMEM((PAIR, 2, ROWS, C), BF), VMEM((PAIR, UNIT, D), BF), VMEM((PAIR, 2, 2, ROWS, C), BF), VMEM((PAIR, 2, UNIT, D), BF),
             VMEM((PAIR, ROWS, C), BF), VMEM((UNIT, D), BF), VMEM((PAIR, ROWS, C), F32), VMEM((UNIT, D), F32),
@@ -699,13 +732,13 @@
             VMEM((PAIR, ROWS_Y, C), BF), VMEM((UNIT_Y, D), BF), VMEM((PAIR, ROWS_Y, C), F32), VMEM((UNIT_Y, D), F32),
             VMEM((PAIR, 2, ROWS_Y, C), BF), VMEM((PAIR, UNIT_Y, D), BF),
             VMEM((PAIR, ROWS_Y, C), BF), VMEM((UNIT_Y, D), BF), VMEM((8, LANES), F32), VMEM((8, 8, LANES), F32),
-            DMA((PAIR, 2)), DMA((PAIR, SLOTS)), DMA, DMA,
+            DMA((PAIR, 2)), DMA((PAIR, SLOTS)), DMA((PAIR,)), DMA, DMA,
             DMA((3, 2)), DMA((3, 2, 2)), DMA((6,)), DMA((ALL,)), DMA((3, ALL)), DMA((7,)), DMA((7,)),
         ],
         compiler_params=pltpu.CompilerParams(vmem_limit_bytes=66_000_000, collective_id=0, has_side_effects=True),
         cost_estimate=pl.CostEstimate(flops=24 * T * D * FF, bytes_accessed=2 * T * FF * 4, transcendentals=0),
         name="backward",
-    )(x, h, dy, kept, gu1, d1, d0)
+    )(h, a0, a1, dy, kept, gu1, d1, d0)
 
 
 def adamw(w, m, v, g):
@@ -746,8 +779,8 @@
 def solution(mesh):
     def step(x, dy, *arrays):
         weights, m, v = (arrays[i : i + 3] for i in (0, 3, 6))
-        h, kept, gu1, d1, d0 = forward(x[0], *weights)
-        ggu, gd, squares = backward(x[0], h, dy[0], kept, gu1, d1, d0)
+        h, a0, a1, kept, gu1, d1, d0 = forward(x[0], *weights)
+        ggu, gd, squares = backward(h, a0, a1, dy[0], kept, gu1, d1, d0)
         return tuple(update(squares, weights, m, v, ggu, gd))
 
     states, cut = P(("rep", "r", "s"), None, None), P(None, "s", None)

time: 457 us -> 440 us (0.963)
  Pallas kernels: 451 us -> 439 us
    pallas_call x2, Pallas kernels: 423 us -> 410 us  [the longest x1 307 us: backward(): pl.pallas_call(backward_kernel, in_specs=[any_] * 8, out_specs=[any_, any...]
where the time goes in v3:
time: 440 us
  Pallas kernels  439 us (100%)
    pallas_call x1, Pallas kernels, backward(): pl.pallas_call(backward_kernel, in_specs=[any_] * 8, out_specs=[any_, any...  307 us
    pallas_call x1, Pallas kernels, forward(): pl.pallas_call(forward_kernel, in_specs=[any_] * 4, out_specs=[any_] * 7,...  103 us
    pallas_call x1, Pallas kernels, update(): pl.pallas_call(update_kernel, grid=(2, N), in_specs=[pl.BlockSpec((8, LAN...  28.6 us

profile of v3, /device:TPU:0, one launch (start us, length us, event | category | flops | bytes accessed | tf_op | source)
XLA Modules:
  0.0 439.5 jit_solution(15721160319105249628)
XLA Ops:
  0.6 102.7 %forward.1 = (bf16[4096,896]{1,0:T(8,128)(2,1)}, bf16[4096,896]{1,0:T(8,128)(2,1)}, bf16[4096,896]{1,0:T(8,128)(2,1)}, f32[9,2,4096,256]{3,2,1,0:T(8,128)}, bf16...) custom-call(bf16[4096,896]{1,0:T(8,128)(2,1)} %bitcast.2, ...), custom_call_target="tpu_custom_call" | custom-call | flops 50734301184 | bytes 75497472 | tf_op jit(solution)/shard_map/forward/pallas_call | solution.py:353
  103.4 307.3 %backward.1 = (bf16[2,9,2,224,256]{4,3,2,1,0:T(8,128)(2,1)}, bf16[2,576,896]{2,1,0:T(8,128)(2,1)}, f32[8,128]{1,0:T(8,128)}) custom-call(bf16[4096,896]{1,0:T(8,128)(2,1)} %get-tuple-element.19.h_ref, bf16[4096,896]{1,0:T(8,128)(2,1)} %get-tuple-element.20.a0_ref, bf16[4096,896]{1,0:T(8,128)(2,1)} %get-tuple-element.21.a1_ref, bf16[4096,896]{1,0:T(8,128)(2,1)} %bitcast.3, ...), custom_call_target="tpu_custom_call" | custom-call | flops 202937204736 | bytes 75497472 | tf_op jit(solution)/shard_map/backward/pallas_call | solution.py:713
  410.7 28.6 %update.1 = (bf16[2,224,2304]{2,1,0:T(8,128)(2,1)}, bf16[2,224,2304]{2,1,0:T(8,128)(2,1)}, bf16[2,576,896]{2,1,0:T(8,128)(2,1)}, f32[2,224,2304]{2,1,0:T(8,128)}...) custom-call(f32[8,128]{1,0:T(8,128)} %get-tuple-element.26.sq, ...), custom_call_target="tpu_custom_call" | custom-call | tf_op jit(solution)/shard_map/update/pallas_call | solution.py:768

commit v4 on v3

--- a/solution.py
+++ b/solution.py
@@ -92,8 +92,8 @@
 
 
 def forward_kernel(
-    x_ref, wg, wu, wd, h_ref, a0_ref, a1_ref, kept, gu1, d1, d0,
-    a, acc, gu, d, keep, hb, ab,
+    x_ref, wg, wu, wd, h_ref, a0_ref, a1_ref, kept, kept_p, gu1, d1, d0,
+    a, acc, gu, d, keep, keep_p, hb, ab,
     lsem, lsemd, ksem, xsem, ssem, rsem, ssemd, rsemd, osem, hsem,
 ):
     x, y, c, at_core, at_x, at_y, _ = where()
@@ -240,7 +240,7 @@
                 keep.at[bank, n], kept.at[kk // GROUPS, :, rows(lax.rem(kk, GROUPS) * SLOTS + n, TB), :], ksem.at[bank, n]
             )
             for n in range(SLOTS)
-        ]
+        ] + [pltpu.make_async_copy(keep_p.at[bank], kept_p.at[kk // GROUPS, rows(lax.rem(kk, GROUPS), GT), :], ksem.at[bank, SLOTS])]
 
     last_chunk = ALL - 1
     save_d0 = pltpu.make_async_copy(d.at[pl.ds(0, N)], d0, osem.at[0, N])
@@ -280,13 +280,22 @@
                 done(keep_copies(kk - 2))
 
             bank = odd(kk)
+
+            def products(n):
+                at = a[rows(k * SLOTS + n, TB), :]
+                return dot(at, gu[j, 0]), dot(at, gu[j, 1])
+
+            ahead = products(0)
             for n in range(SLOTS):
                 s = rows(k * SLOTS + n, TB)
-                at = a[s, :]
-                gate, up = dot(at, gu[j, 0]), dot(at, gu[j, 1])
-                keep[bank, n, 0] = gate
-                keep[bank, n, 1] = up
-                p = (silu(gate)[0] * up).astype(BF)
+                gate, up = ahead
+                if n + 1 < SLOTS:
+                    ahead = products(n + 1)
+                silu_, slope = silu(gate)
+                keep[bank, n, 0] = up * slope
+                keep[bank, n, 1] = silu_
+                p = (silu_ * up).astype(BF)
+                keep_p[bank, pl.ds(n * TB, TB), :] = p
                 acc[s, :] += dot(p, d[j])
             go(keep_copies(kk))
             return 0
@@ -353,10 +362,11 @@
     return pl.pallas_call(
         forward_kernel,
         in_specs=[any_] * 4,
-        out_specs=[any_] * 7,
+        out_specs=[any_] * 8,
         out_shape=[
             *[jax.ShapeDtypeStruct((T, D), BF)] * 3,
             jax.ShapeDtypeStruct((N, 2, T, C), F32),
+            jax.ShapeDtypeStruct((N, T, C), BF),
             jax.ShapeDtypeStruct((N, 2, D, C), BF),
             jax.ShapeDtypeStruct((N, C, D), BF),
             jax.ShapeDtypeStruct((N, C, D), BF),
@@ -367,8 +377,9 @@
             VMEM((ALL, 2, D, C), BF),
             VMEM((ALL, C, D), BF),
             VMEM((PAIR, SLOTS, 2, TB, C), F32),
+            VMEM((PAIR, GT, C), BF),
             *[VMEM((PAIR, EB, D), BF)] * 2,
-            DMA((ALL, 2, 2)), DMA((ALL, 2)), DMA((PAIR, SLOTS)), DMA,
+            DMA((ALL, 2, 2)), DMA((ALL, 2)), DMA((PAIR, SLOTS + 1)), DMA,
             DMA((5, ALL)), DMA((5, ALL)), DMA((5, ALL, 2)), DMA((5, ALL, 2)), DMA((PAIR, N + 1)), DMA((PAIR, PAIR)),
         ],
         compiler_params=pltpu.CompilerParams(vmem_limit_bytes=66_000_000, collective_id=1, has_side_effects=True),
@@ -378,7 +389,7 @@
 
 
 def backward_kernel(
-    h_ref, a0_ref, a1_ref, dy_ref, kept, gu1, d1, d0,
+    h_ref, a0_ref, a1_ref, dy_ref, kept, kept_p, gu1, d1, d0,
     ggu, gd, sq_out,
     a, dy, acc, terms, bgu, bd, keep, hb, res, resd,
     s1, s1d, r1, r1d, s2, s2d, own2, own2d, r2, r2d, s3, s3d, own3, own3d, r3, r3d, fin, find, sq, sqr,
@@ -574,11 +585,18 @@
         done(weights(j, slot))
 
         def some(group, _):
+            def products(n):
+                s = rows(group * SLOTS + n, TB)
+                at = a[s, :]
+                return dot(at, bgu[slot, 0]), dot(at, bgu[slot, 1]), dot(dy[s, :], bd[slot], 1, 1)
+
+            ahead = products(0)
             for n in range(SLOTS):
                 s, b = rows(group * SLOTS + n, TB), pl.ds(n * TB, TB)
-                at = a[s, :]
-                gate, up = dot(at, bgu[slot, 0]), dot(at, bgu[slot, 1])
-                dp = dot(dy[s, :], bd[slot], 1, 1).astype(BF).astype(F32)
+                gate, up, dp = ahead
+                dp = dp.astype(BF).astype(F32)
+                if n + 1 < SLOTS:
+                    ahead = products(n + 1)
                 if n < 3:
                     gradient(n, 1 - group, odd(slot + 1 + group))
                 silu_, slope = silu(gate)
@@ -643,17 +661,18 @@
         done(weights0(j, slot))
         out = lax.rem(N + j, 2)
         def some(group, _):
+            product = pltpu.make_async_copy(kept_p.at[j, rows(group, GT), :], terms.at[group, DOWN], ksem.at[group, SLOTS])
+            product.start()
             done(kept_copies(j, group))
             for n in range(SLOTS):
                 s, b = rows(group * SLOTS + n, TB), pl.ds(n * TB, TB)
                 dp = dot(dy[s, :], bd[slot], 1, 1).astype(BF).astype(F32)
                 if n < 3:
                     gradient(n, 1 - group, odd(out + 1 + group))
-                gate, up = keep[group, n, 0], keep[group, n, 1]
-                silu_, slope = silu(gate)
-                terms[group, 2, b, :] = (silu_ * up).astype(BF)
-                terms[group, 0, b, :] = (dp * up * slope).astype(BF)
-                terms[group, 1, b, :] = (dp * silu_).astype(BF)
+                terms[group, 0, b, :] = (dp * keep[group, n, 0]).astype(BF)
+                terms[group, 1, b, :] = (dp * keep[group, n, 1]).astype(BF)
+
+            product.wait()
 
             @pl.when(j + 1 < N)
             def _():
@@ -708,11 +727,11 @@
     sq_out[...] = functools.reduce(lambda t, k: t + sqr[k], range(1, 8), sqr[0])
 
 
-def backward(h, a0, a1, dy, kept, gu1, d1, d0):
+def backward(h, a0, a1, dy, kept, kept_p, gu1, d1, d0):
     any_ = pl.BlockSpec(memory_space=ANY)
     return pl.pallas_call(
         backward_kernel,
-        in_specs=[any_] * 8,
+        in_specs=[any_] * 9,
         out_specs=[any_, any_, pl.BlockSpec(memory_space=VMEM)],
         out_shape=[
             jax.ShapeDtypeStruct((2, N, 2, ROWS, C), BF),
@@ -732,13 +751,13 @@
             VMEM((PAIR, ROWS_Y, C), BF), VMEM((UNIT_Y, D), BF), VMEM((PAIR, ROWS_Y, C), F32), VMEM((UNIT_Y, D), F32),
             VMEM((PAIR, 2, ROWS_Y, C), BF), VMEM((PAIR, UNIT_Y, D), BF),
             VMEM((PAIR, ROWS_Y, C), BF), VMEM((UNIT_Y, D), BF), VMEM((8, LANES), F32), VMEM((8, 8, LANES), F32),
-            DMA((PAIR, 2)), DMA((PAIR, SLOTS)), DMA((PAIR,)), DMA, DMA,
+            DMA((PAIR, 2)), DMA((PAIR, SLOTS + 1)), DMA((PAIR,)), DMA, DMA,
             DMA((3, 2)), DMA((3, 2, 2)), DMA((6,)), DMA((ALL,)), DMA((3, ALL)), DMA((7,)), DMA((7,)),
         ],
         compiler_params=pltpu.CompilerParams(vmem_limit_bytes=66_000_000, collective_id=0, has_side_effects=True),
         cost_estimate=pl.CostEstimate(flops=24 * T * D * FF, bytes_accessed=2 * T * FF * 4, transcendentals=0),
         name="backward",
-    )(h, a0, a1, dy, kept, gu1, d1, d0)
+    )(h, a0, a1, dy, kept, kept_p, gu1, d1, d0)
 
 
 def adamw(w, m, v, g):
@@ -779,8 +798,8 @@
 def solution(mesh):
     def step(x, dy, *arrays):
         weights, m, v = (arrays[i : i + 3] for i in (0, 3, 6))
-        h, a0, a1, kept, gu1, d1, d0 = forward(x[0], *weights)
-        ggu, gd, squares = backward(h, a0, a1, dy[0], kept, gu1, d1, d0)
+        h, a0, a1, kept, kept_p, gu1, d1, d0 = forward(x[0], *weights)
+        ggu, gd, squares = backward(h, a0, a1, dy[0], kept, kept_p, gu1, d1, d0)
         return tuple(update(squares, weights, m, v, ggu, gd))
 
     states, cut = P(("rep", "r", "s"), None, None), P(None, "s", None)

time: 440 us -> 437 us (level)
  no operation moved by 1% of the time
where the time goes in v4:
time: 437 us; the launch traced here: 436 us
  Pallas kernels  435 us (100%)
    pallas_call x1, Pallas kernels, backward(): pl.pallas_call(backward_kernel, in_specs=[any_] * 9, out_specs=[any_, any...  301 us
    pallas_call x1, Pallas kernels, forward(): pl.pallas_call(forward_kernel, in_specs=[any_] * 4, out_specs=[any_] * 8,...  105 us
    pallas_call x1, Pallas kernels, update(): pl.pallas_call(update_kernel, grid=(2, N), in_specs=[pl.BlockSpec((8, LAN...  28.6 us

profile of v4, /device:TPU:0, one launch (start us, length us, event | category | flops | bytes accessed | tf_op | source)
XLA Modules:
  0.0 436.2 jit_solution(7756173012535540997)
XLA Ops:
  0.6 105.3 %forward.1 = (bf16[4096,896]{1,0:T(8,128)(2,1)}, bf16[4096,896]{1,0:T(8,128)(2,1)}, bf16[4096,896]{1,0:T(8,128)(2,1)}, f32[9,2,4096,256]{3,2,1,0:T(8,128)}, bf16...) custom-call(bf16[4096,896]{1,0:T(8,128)(2,1)} %bitcast.2, ...), custom_call_target="tpu_custom_call" | custom-call | flops 50734301184 | bytes 75497472 | tf_op jit(solution)/shard_map/forward/pallas_call | solution.py:362
  106.0 301.4 %backward.1 = (bf16[2,9,2,224,256]{4,3,2,1,0:T(8,128)(2,1)}, bf16[2,576,896]{2,1,0:T(8,128)(2,1)}, f32[8,128]{1,0:T(8,128)}) custom-call(bf16[4096,896]{1,0:T(8,128)(2,1)} %get-tuple-element.20.h_ref, bf16[4096,896]{1,0:T(8,128)(2,1)} %get-tuple-element.21.a0_ref, bf16[4096,896]{1,0:T(8,128)(2,1)} %get-tuple-element.22.a1_ref, bf16[4096,896]{1,0:T(8,128)(2,1)} %bitcast.3, ...), custom_call_target="tpu_custom_call" | custom-call | flops 202937204736 | bytes 75497472 | tf_op jit(solution)/shard_map/backward/pallas_call | solution.py:732
  407.4 28.6 %update.1 = (bf16[2,224,2304]{2,1,0:T(8,128)(2,1)}, bf16[2,224,2304]{2,1,0:T(8,128)(2,1)}, bf16[2,576,896]{2,1,0:T(8,128)(2,1)}, f32[2,224,2304]{2,1,0:T(8,128)}...) custom-call(f32[8,128]{1,0:T(8,128)} %get-tuple-element.28.sq, ...), custom_call_target="tpu_custom_call" | custom-call | tf_op jit(solution)/shard_map/update/pallas_call | solution.py:787
